TPU v7x, 256 devices: a whole 4x4x8 slice. The times are simulated.
256 devices in a mesh: pencil: 64 (over y, x_lo, z), angle: 4 (over x_hi, core).
Axes of the slice: x: 4 (x_hi: 2, x_lo: 2; x = x_hi * 2 + x_lo), y: 4, z: 8, core: 2. Of those that a mesh axis runs over, the one named last changes fastest.
Arguments:
- tomo_real: bfloat16 [512, 512, 128], P(None, 'pencil'), may hold values from -6 to 6
- tomo_imag: bfloat16 [512, 512, 128], P(None, 'pencil'), may hold values from -6 to 6
- template_real: bfloat16 [8, 512, 512, 128], P('angle', None, 'pencil'), may hold values from -6 to 6
- template_imag: bfloat16 [8, 512, 512, 128], P('angle', None, 'pencil'), may hold values from -6 to 6
- wedge_flags: int32 [512, 512, 128], P(None, 'pencil'), may hold values 0 or 1
- local_sigma: float32 [512, 512, 128], P('pencil'), may hold values from 0.5 to 2
Outputs:
- best_score: float32 [512, 512, 128], P('pencil', 'angle')
- runner_up: float32 [512, 512, 128], P('pencil', 'angle')
All inputs are finite; a program needn't handle non-finite values. No bound on the sum of `wedge_flags` on one device may be relied on, other than what follows from the above.
Results may differ from a plain program's by a relative error of at most 0.0064.
Values may be sent and summed in bfloat16 or wider, within the bound.
No kernel may reach another device: no remote copies, remote signals or barrier semaphores. Data moves between devices by JAX's collectives and lax.ppermute only.
A program may use at most 128 MiB of HBM per device.

v0:
```python
import math

import jax
import jax.numpy as jnp
import numpy as np
from jax import lax
from jax.experimental import pallas as pl
from jax.experimental.pallas import tpu as pltpu
from jax.sharding import PartitionSpec as P

CHUNKS = (4, 4)
CORE = ((0, 1), (1, 0), (2, 3), (3, 2))
FAR = ((0, 2), (1, 3), (2, 0), (3, 1))


def phases(length):
    k = np.arange(length, dtype=np.int64)
    angle = (k[:, None] * k[None, :] % length) * (2.0 * math.pi / length)
    return np.cos(angle), np.sin(angle)


def z_table(size_z):
    cos, sin = phases(size_z)
    return np.block([[cos, sin], [-sin, cos]]).astype(jnp.bfloat16)


def x_table(size_x, groups, first, count):
    cos, sin = phases(size_x)
    each = size_x // groups
    rows = (np.arange(groups)[:, None] * each + np.arange(first, first + count)[None, :]).reshape(-1)
    return np.concatenate([cos[rows], sin[rows]], 0).astype(jnp.bfloat16)


def y_table(size_y, groups):
    cos, sin = phases(size_y)
    both = np.stack([cos.reshape(size_y, groups, -1), -sin.reshape(size_y, groups, -1)], 2)
    return both.reshape(size_y, -1).astype(jnp.bfloat16)


def along_z(tr, ti, ar, ai, flags, table, out, tmp):
    block, rows, size_z = tr.shape
    flag = flags[...].astype(jnp.float32)
    fr = tr[...].astype(jnp.float32) * flag
    fi = ti[...].astype(jnp.float32) * flag
    for a in range(ar.shape[0]):
        br = ar[a].astype(jnp.float32)
        bi = ai[a].astype(jnp.float32)
        pr = (fr * br + fi * bi).astype(jnp.bfloat16).reshape(block * rows, size_z)
        pi = (fi * br - fr * bi).astype(jnp.bfloat16).reshape(block * rows, size_z)
        both = jnp.concatenate([pr, pi], 1)
        sums = jnp.dot(both, table[...], preferred_element_type=jnp.float32)
        tmp[2 * a] = sums[:, :size_z]
        tmp[2 * a + 1] = sums[:, size_z:]
        for k in range(rows):
            half = [tmp[2 * a + h, pl.ds(k, block, stride=rows), :] for h in range(2)]
            out[a, k] = jnp.concatenate(half, 1).astype(jnp.bfloat16)


def along_x(q, table, out, tmp):
    rows, _, width = q.shape[1:]
    size_z = width // 2
    half = table.shape[0] // 2

    def one(k, carry):
        both = jnp.dot(table[...], q[0, k], preferred_element_type=jnp.float32)
        tmp[pl.ds(k, half, stride=2 * rows), :] = both[:half, :size_z] - both[half:, size_z:]
        tmp[pl.ds(k + rows, half, stride=2 * rows), :] = both[half:, :size_z] + both[:half, size_z:]
        return carry

    lax.fori_loop(0, rows, one, 0)
    out[...] = tmp[...].astype(jnp.bfloat16).reshape(out.shape)


def along_y(who, got, sigma, table, keep, send, *, scale):
    groups, angles, count, pair, size_z = got.shape
    me = who[0]
    part = table.shape[0] // 4
    starts = [pl.multiple_of(jnp.bitwise_xor(me, r) * part, part) for r in range(4)]
    left = jnp.concatenate([table[pl.ds(s, part), :] for s in starts], 0)
    sums = []
    for a in range(angles):
        right = jnp.concatenate([got[:, a, i].reshape(groups * pair, size_z) for i in range(count)], 1)
        sums.append(jnp.dot(left, right, preferred_element_type=jnp.float32))
    for i in range(count):
        for r in range(4):
            here = (slice(r * part, (r + 1) * part), slice(i * size_z, (i + 1) * size_z))
            inverse = scale / sigma[i, pl.ds(starts[r], part), :]
            best = sums[0][here] * inverse
            runner = jnp.full_like(best, -1e30)
            for a in range(1, angles):
                score = sums[a][here] * inverse
                runner = jnp.maximum(runner, jnp.minimum(best, score))
                best = jnp.maximum(best, score)
            to = send if r % 2 else keep
            to[r // 2, 0, i] = best.astype(jnp.bfloat16)
            to[r // 2, 1, i] = runner.astype(jnp.bfloat16)


def top_two(first, later):
    best = jnp.maximum(first[0], later[0])
    return best, jnp.maximum(jnp.minimum(first[0], later[0]), jnp.maximum(first[1], later[1]))


def join_core(mine, other, keep, send):
    for slot, to in enumerate((keep, send)):
        best, runner = top_two((mine[slot, 0], mine[slot, 1]), (other[slot, 0], other[slot, 1]))
        to[0] = best
        to[1] = runner


def join_far(*refs):
    parts, (best_out, runner_out) = refs[:-2], refs[-2:]
    at = 0
    for mine, other in zip(parts[::2], parts[1::2]):
        best, runner = top_two((mine[0], mine[1]), (other[0], other[1]))
        best_out[at : at + mine.shape[1]] = best.astype(jnp.float32)
        runner_out[at : at + mine.shape[1]] = runner.astype(jnp.float32)
        at += mine.shape[1]


def cost(flops, moved):
    return pl.CostEstimate(flops=flops, bytes_accessed=moved, transcendentals=0)


def on_device(tomo_real, tomo_imag, template_real, template_imag, wedge_flags, local_sigma):
    size_x, rows, size_z = tomo_real.shape
    angles = template_real.shape[0]
    size_y = local_sigma.shape[1]
    groups = size_y // rows
    part = size_y // 4
    scale = 1.0 / math.sqrt(size_x * size_y * size_z)
    block = 64
    params = pltpu.CompilerParams(vmem_limit_bytes=48 * 1024 * 1024)

    spectrum = pl.pallas_call(
        along_z,
        grid=(size_x // block,),
        in_specs=[
            pl.BlockSpec((block, rows, size_z), lambda i: (i, 0, 0)),
            pl.BlockSpec((block, rows, size_z), lambda i: (i, 0, 0)),
            pl.BlockSpec((angles, block, rows, size_z), lambda i: (0, i, 0, 0)),
            pl.BlockSpec((angles, block, rows, size_z), lambda i: (0, i, 0, 0)),
            pl.BlockSpec((block, rows, size_z), lambda i: (i, 0, 0)),
            pl.BlockSpec((2 * size_z, 2 * size_z), lambda i: (0, 0)),
        ],
        out_specs=pl.BlockSpec((angles, rows, block, 2 * size_z), lambda i: (0, 0, i, 0)),
        out_shape=jax.ShapeDtypeStruct((angles, rows, size_x, 2 * size_z), jnp.bfloat16),
        scratch_shapes=[pltpu.VMEM((2 * angles, block * rows, size_z), jnp.float32)],
        compiler_params=params,
        cost_estimate=cost(8 * angles * size_x * rows * size_z * size_z, 12 * 2**20),
        name="along_z",
    )(tomo_real, tomo_imag, template_real, template_imag, wedge_flags, z_table(size_z))

    me = lax.axis_index("angle").astype(jnp.int32)[None]
    columns = y_table(size_y, groups)
    first = 0
    sent = []
    for count in CHUNKS:
        table = x_table(size_x, groups, first, count)
        sent.append(
            pl.pallas_call(
                along_x,
                grid=(angles,),
                in_specs=[
                    pl.BlockSpec((1, rows, size_x, 2 * size_z), lambda a: (a, 0, 0, 0)),
                    pl.BlockSpec(table.shape, lambda a: (0, 0)),
                ],
                out_specs=pl.BlockSpec((groups, 1, count, 2 * rows, size_z), lambda a: (0, a, 0, 0, 0)),
                out_shape=jax.ShapeDtypeStruct((groups, angles, count, 2 * rows, size_z), jnp.bfloat16),
                scratch_shapes=[pltpu.VMEM((groups * count * 2 * rows, size_z), jnp.float32)],
                compiler_params=params,
                cost_estimate=cost(8 * angles * size_x * groups * count * rows * size_z, 8 * 2**20),
                name="along_x",
            )(spectrum, table)
        )
        first += count

    joined = []
    first = 0
    for count, piece in zip(CHUNKS, sent):
        got = lax.all_to_all(piece, "pencil", split_axis=0, concat_axis=0, tiled=True)
        offset = first // 2
        out = jax.ShapeDtypeStruct((2, 2, count, part, size_z), jnp.bfloat16)
        keep, send = pl.pallas_call(
            lambda *refs: along_y(*refs, scale=scale),
            grid=(count // 2,),
            in_specs=[
                pl.BlockSpec(memory_space=pltpu.SMEM),
                pl.BlockSpec((groups, angles, 2, 2 * rows, size_z), lambda i: (0, 0, i, 0, 0)),
                pl.BlockSpec((2, size_y, size_z), lambda i, offset=offset: (i + offset, 0, 0)),
                pl.BlockSpec(columns.shape, lambda i: (0, 0)),
            ],
            out_specs=[pl.BlockSpec((2, 2, 2, part, size_z), lambda i: (0, 0, i, 0, 0))] * 2,
            out_shape=[out, out],
            compiler_params=params,
            cost_estimate=cost(4 * angles * count * size_y * size_y * size_z, 2 * 2**20 * count),
            name="along_y",
        )(me, got, local_sigma, columns)
        other = lax.ppermute(send, "angle", CORE)
        near = jax.ShapeDtypeStruct((2, count, part, size_z), jnp.bfloat16)
        keep, send = pl.pallas_call(
            join_core,
            out_shape=[near, near],
            compiler_params=params,
            cost_estimate=cost(2**20 * count, 2**19 * count),
            name="join_core",
        )(keep, other)
        joined += [keep, lax.ppermute(send, "angle", FAR)]
        first += count

    done = jax.ShapeDtypeStruct((local_sigma.shape[0], part, size_z), jnp.float32)
    return tuple(
        pl.pallas_call(
            join_far,
            out_shape=[done, done],
            compiler_params=params,
            cost_estimate=cost(2**20, 2**21),
            name="join_far",
        )(*joined)
    )


def solution(mesh):
    in_specs = (
        P(None, "pencil", None),
        P(None, "pencil", None),
        P("angle", None, "pencil", None),
        P("angle", None, "pencil", None),
        P(None, "pencil", None),
        P("pencil", None, None),
    )
    out_specs = (P("pencil", "angle", None), P("pencil", "angle", None))
    return jax.shard_map(
        on_device, mesh=mesh, in_specs=in_specs, out_specs=out_specs, check_vma=False
    )
```

profile of v0, /device:TPU:1, one launch (start us, length us, event | category | flops | bytes accessed | tf_op | source)
XLA Modules:
  0.0 166.1 jit_solution(14641556629949542483)
XLA Ops:
  0.6 0.0 copy-start.3
  0.6 1.6 copy-done.3
  2.2 0.0 copy-start.6
  2.2 1.2 copy-done.6
  3.4 0.0 copy-start.7
  3.5 1.2 copy-done.7
  4.7 0.0 copy-start.10
  4.7 0.9 copy-done.10
  5.6 0.0 copy-start.12
  5.6 8.1 %along_z.1.q = bf16[2,8,512,256]{3,2,1,0:T(8,128)(2,1)} custom-call(bf16[512,8,128]{2,1,0:T(8,128)(2,1)S(1)} %copy-done.6, bf16[512,8,128]{2,1,0:T(8,128)(2,1)S(1)} %copy-done.7, bf16[2,512,8,128]{3,2,1,0:T(8,128)(2,1)S(1)} %copy-done.3, bf16[2,512,8,128]{3,2,1,0:T(8,128)(2,1)} %ai.1, s32[512,8,128]{2,1,0:T(8,128)} %flags.1, bf16[256,256]{1,0:T(8,128)(2,1)S(1)} %copy-done.10), custom_call_target="tpu_custom_call" | custom-call | flops 1073741824 | bytes 12582912 | tf_op jit(solution)/shard_map/along_z/pallas_call | solution.py:135
  13.7 0.0 copy-done.12
  13.7 7.2 %along_x.3 = bf16[64,2,4,16,128]{4,3,2,1,0:T(8,128)(2,1)S(1)} custom-call(bf16[2,8,512,256]{3,2,1,0:T(8,128)(2,1)} %along_z.1.q, bf16[512,512]{1,0:T(8,128)(2,1)S(1)} %copy-done.12), custom_call_target="tpu_custom_call" | custom-call | flops 2147483648 | bytes 8388608 | tf_op jit(solution)/shard_map/along_x/pallas_call | solution.py:161
  20.9 0.0 copy-start.5
  20.9 1.3 copy-done.5
  22.2 0.0 copy-start.11
  22.2 13.7 %all-to-all-start.1 = ((bf16[64,2,4,16,128]{4,3,2,1,0:T(8,128)(2,1)}), bf16[64,2,4,16,128]{4,3,2,1,0:T(8,128)(2,1)S(1)}, u32[]{:S(2)}, u32[]{:S(2)}) async-start(bf16[64,2,4,16,128]{4,3,2,1,0:T(8,128)(2,1)} %copy-done.5), calls=%async_computation.1 | async-start | bytes 4194304 | tf_op jit(solution)/shard_map/all_to_all | solution.py:181
  35.9 0.0 copy-done.11
  36.0 7.2 %along_x.2 = bf16[64,2,4,16,128]{4,3,2,1,0:T(8,128)(2,1)S(1)} custom-call(bf16[2,8,512,256]{3,2,1,0:T(8,128)(2,1)} %along_z.1.q, bf16[512,512]{1,0:T(8,128)(2,1)S(1)} %copy-done.11), custom_call_target="tpu_custom_call" | custom-call | flops 2147483648 | bytes 8388608 | tf_op jit(solution)/shard_map/along_x/pallas_call | solution.py:161
  43.2 0.0 copy-start.4
  43.2 1.3 copy-done.4
  44.5 0.0 copy-start.2
  44.5 39.0 %all-to-all-done.1.refs_1_ = bf16[64,2,4,16,128]{4,3,2,1,0:T(8,128)(2,1)S(1)} async-done(((bf16[64,2,4,16,128]{4,3,2,1,0:T(8,128)(2,1)}), bf16[64,2,4,16,128]{4,3,2,1,0:T(8,128)(2,1)S(1)}, u32[]{:S(2)}, u32[]{:S(2)}) %all-to-all-start.1) | async-done | bytes 2097184 | tf_op jit(solution)/shard_map/all_to_all | solution.py:181
  83.6 0.0 copy-start
  83.6 1.3 copy-done
  84.9 9.1 %all-to-all-start = ((bf16[64,2,4,16,128]{4,3,2,1,0:T(8,128)(2,1)}), bf16[64,2,4,16,128]{4,3,2,1,0:T(8,128)(2,1)S(1)}, u32[]{:S(2)}, u32[]{:S(2)}) async-start(bf16[64,2,4,16,128]{4,3,2,1,0:T(8,128)(2,1)} %copy-done.4), calls=%async_computation | async-start | bytes 4194304 | tf_op jit(solution)/shard_map/all_to_all | solution.py:181
  94.0 0.0 copy-done.2
  94.0 0.0 copy-start.1
  94.0 1.6 copy-done.1
  95.6 3.3 %along_y.3 = (bf16[2,2,4,128,128]{4,3,2,1,0:T(8,128)(2,1)S(1)}, bf16[2,2,4,128,128]{4,3,2,1,0:T(8,128)(2,1)}) custom-call(s32[1]{0:T(128)} %bitcast.refs_0_, bf16[64,2,4,16,128]{4,3,2,1,0:T(8,128)(2,1)S(1)} %copy-done.1, f32[8,512,128]{2,1,0:T(8,128)} %refs_2_.3, bf16[512,1024]{1,0:T(8,128)(2,1)S(1)} %copy-done.2), custom_call_target="tpu_custom_call" | custom-call | flops 1073741824 | bytes 8388608 | tf_op jit(solution)/shard_map/along_y/pallas_call | solution.py:184
  98.8 0.0 copy-start.8
  98.8 0.8 copy-done.8
  99.6 1.7 %collective-permute-start.2 = (bf16[2,2,4,128,128]{4,3,2,1,0:T(8,128)(2,1)}, bf16[2,2,4,128,128]{4,3,2,1,0:T(8,128)(2,1)}, u32[]{:S(2)}, u32[]{:S(2)}) collective-permute-start(bf16[2,2,4,128,128]{4,3,2,1,0:T(8,128)(2,1)} %get-tuple-element.15), channel_id=1, source_target_pairs={{0,1},{1,0},{2,3},{3,2},{4,5},{5,4},{6,7},{7,6},{8,9},{9,8},{10,11... | collective-permute-start | bytes 1572872 | tf_op jit(solution)/shard_map/ppermute | solution.py:199
  101.4 39.4 %all-to-all-done.refs_1_ = bf16[64,2,4,16,128]{4,3,2,1,0:T(8,128)(2,1)S(1)} async-done(((bf16[64,2,4,16,128]{4,3,2,1,0:T(8,128)(2,1)}), bf16[64,2,4,16,128]{4,3,2,1,0:T(8,128)(2,1)S(1)}, u32[]{:S(2)}, u32[]{:S(2)}) %all-to-all-start) | async-done | bytes 2097184 | tf_op jit(solution)/shard_map/all_to_all | solution.py:181
  140.8 0.0 copy-start.9
  140.8 2.7 %along_y.2 = (bf16[2,2,4,128,128]{4,3,2,1,0:T(8,128)(2,1)S(1)}, bf16[2,2,4,128,128]{4,3,2,1,0:T(8,128)(2,1)S(1)}) custom-call(s32[1]{0:T(128)} %bitcast.refs_0_, bf16[64,2,4,16,128]{4,3,2,1,0:T(8,128)(2,1)S(1)} %all-to-all-done.refs_1_, f32[8,512,128]{2,1,0:T(8,128)} %refs_2_.3, bf16[512,1024]{1,0:T(8,128)(2,1)S(1)} %copy-done.2), custom_call_target="tpu_custom_call" | custom-call | flops 1073741824 | bytes 8388608 | tf_op jit(solution)/shard_map/along_y/pallas_call | solution.py:184
  143.5 5.3 %collective-permute-start = (bf16[2,2,4,128,128]{4,3,2,1,0:T(8,128)(2,1)S(1)}, bf16[2,2,4,128,128]{4,3,2,1,0:T(8,128)(2,1)S(1)}, u32[]{:S(2)}, u32[]{:S(2)}) collective-permute-start(bf16[2,2,4,128,128]{4,3,2,1,0:T(8,128)(2,1)S(1)} %get-tuple-element.11), channel_id=1, source_target_pairs={{0,1},{1,0},{2,3},{3,2},{4,5},{5,4},{6,7},{7,6},{8,9},{9,8},{10,11... | collective-permute-start | bytes 1572872 | tf_op jit(solution)/shard_map/ppermute | solution.py:199
  148.8 0.0 collective-permute-done.2.other
  148.8 0.0 copy-done.9
  148.8 1.2 join_core.3
  150.0 2.5 %collective-permute-start.3 = (bf16[2,4,128,128]{3,2,1,0:T(8,128)(2,1)S(1)}, bf16[2,4,128,128]{3,2,1,0:T(8,128)(2,1)S(1)}, u32[]{:S(2)}, u32[]{:S(2)}) collective-permute-start(bf16[2,4,128,128]{3,2,1,0:T(8,128)(2,1)S(1)} %get-tuple-element.17), channel_id=1, source_target_pairs={{0,2},{1,3},{2,0},{3,1},{4,6},{5,7},{6,4},{7,5},{8,10},{9,11},{10,... | collective-permute-start | bytes 786440 | tf_op jit(solution)/shard_map/ppermute | solution.py:208
  152.5 0.0 collective-permute-done.other
  152.5 0.2 join_core.2
  152.7 0.6 collective-permute-start.1
  153.3 6.1 %collective-permute-done.3.refs_3_ = bf16[2,4,128,128]{3,2,1,0:T(8,128)(2,1)S(1)} collective-permute-done((bf16[2,4,128,128]{3,2,1,0:T(8,128)(2,1)S(1)}, bf16[2,4,128,128]{3,2,1,0:T(8,128)(2,1)S(1)}, u32[]{:S(2)}, u32[]{:S(2)}) %collective-permute-start.3) | collective-permute-done | bytes 262176 | tf_op jit(solution)/shard_map/ppermute | solution.py:208
  159.4 5.6 %collective-permute-done.1.refs_1_ = bf16[2,4,128,128]{3,2,1,0:T(8,128)(2,1)S(1)} collective-permute-done((bf16[2,4,128,128]{3,2,1,0:T(8,128)(2,1)S(1)}, bf16[2,4,128,128]{3,2,1,0:T(8,128)(2,1)S(1)}, u32[]{:S(2)}, u32[]{:S(2)}) %collective-permute-start.1) | collective-permute-done | bytes 262176 | tf_op jit(solution)/shard_map/ppermute | solution.py:208
  165.0 1.1 join_far.1
Async XLA Ops:
  0.6 1.6 copy-start.3
  2.2 1.2 copy-start.6
  3.4 1.2 copy-start.7
  4.7 0.9 copy-start.10
  5.6 8.1 %copy-start.12 = (bf16[512,512]{1,0:T(8,128)(2,1)S(1)}, bf16[512,512]{1,0:T(8,128)(2,1)}, u32[]{:S(2)}) copy-start(bf16[512,512]{1,0:T(8,128)(2,1)} %constant.14.clone.table) | copy-start | bytes 1572868
  20.9 1.3 copy-start.5
  22.2 13.7 %copy-start.11 = (bf16[512,512]{1,0:T(8,128)(2,1)S(1)}, bf16[512,512]{1,0:T(8,128)(2,1)}, u32[]{:S(2)}) copy-start(bf16[512,512]{1,0:T(8,128)(2,1)} %constant.13.clone.table) | copy-start | bytes 1572868
  22.2 61.3 %all-to-all-start.1 = ((bf16[64,2,4,16,128]{4,3,2,1,0:T(8,128)(2,1)}), bf16[64,2,4,16,128]{4,3,2,1,0:T(8,128)(2,1)S(1)}, u32[]{:S(2)}, u32[]{:S(2)}) async-start(bf16[64,2,4,16,128]{4,3,2,1,0:T(8,128)(2,1)} %copy-done.5), calls=%async_computation.1 | async-start | bytes 4194304 | tf_op jit(solution)/shard_map/all_to_all | solution.py:181
  43.2 1.3 copy-start.4
  44.5 49.4 %copy-start.2 = (bf16[512,1024]{1,0:T(8,128)(2,1)S(1)}, bf16[512,1024]{1,0:T(8,128)(2,1)}, u32[]{:S(2)}) copy-start(bf16[512,1024]{1,0:T(8,128)(2,1)} %constant.15.clone.refs_3_) | copy-start | bytes 3145732
  83.6 1.3 copy-start
  84.9 55.9 %all-to-all-start = ((bf16[64,2,4,16,128]{4,3,2,1,0:T(8,128)(2,1)}), bf16[64,2,4,16,128]{4,3,2,1,0:T(8,128)(2,1)S(1)}, u32[]{:S(2)}, u32[]{:S(2)}) async-start(bf16[64,2,4,16,128]{4,3,2,1,0:T(8,128)(2,1)} %copy-done.4), calls=%async_computation | async-start | bytes 4194304 | tf_op jit(solution)/shard_map/all_to_all | solution.py:181
  94.0 1.6 copy-start.1
  98.8 0.8 copy-start.8
  99.6 49.1 %collective-permute-start.2 = (bf16[2,2,4,128,128]{4,3,2,1,0:T(8,128)(2,1)}, bf16[2,2,4,128,128]{4,3,2,1,0:T(8,128)(2,1)}, u32[]{:S(2)}, u32[]{:S(2)}) collective-permute-start(bf16[2,2,4,128,128]{4,3,2,1,0:T(8,128)(2,1)} %get-tuple-element.15), channel_id=1, source_target_pairs={{0,1},{1,0},{2,3},{3,2},{4,5},{5,4},{6,7},{7,6},{8,9},{9,8},{10,11... | collective-permute-start | bytes 1572872 | tf_op jit(solution)/shard_map/ppermute | solution.py:199
  140.8 8.0 %copy-start.9 = (bf16[2,2,4,128,128]{4,3,2,1,0:T(8,128)(2,1)S(1)}, bf16[2,2,4,128,128]{4,3,2,1,0:T(8,128)(2,1)}, u32[]{:S(2)}) copy-start(bf16[2,2,4,128,128]{4,3,2,1,0:T(8,128)(2,1)} %copy-done.8) | copy-start | bytes 1572868
  143.5 9.0 %collective-permute-start = (bf16[2,2,4,128,128]{4,3,2,1,0:T(8,128)(2,1)S(1)}, bf16[2,2,4,128,128]{4,3,2,1,0:T(8,128)(2,1)S(1)}, u32[]{:S(2)}, u32[]{:S(2)}) collective-permute-start(bf16[2,2,4,128,128]{4,3,2,1,0:T(8,128)(2,1)S(1)} %get-tuple-element.11), channel_id=1, source_target_pairs={{0,1},{1,0},{2,3},{3,2},{4,5},{5,4},{6,7},{7,6},{8,9},{9,8},{10,11... | collective-permute-start | bytes 1572872 | tf_op jit(solution)/shard_map/ppermute | solution.py:199
  150.0 9.4 %collective-permute-start.3 = (bf16[2,4,128,128]{3,2,1,0:T(8,128)(2,1)S(1)}, bf16[2,4,128,128]{3,2,1,0:T(8,128)(2,1)S(1)}, u32[]{:S(2)}, u32[]{:S(2)}) collective-permute-start(bf16[2,4,128,128]{3,2,1,0:T(8,128)(2,1)S(1)} %get-tuple-element.17), channel_id=1, source_target_pairs={{0,2},{1,3},{2,0},{3,1},{4,6},{5,7},{6,4},{7,5},{8,10},{9,11},{10,... | collective-permute-start | bytes 786440 | tf_op jit(solution)/shard_map/ppermute | solution.py:208
  152.7 12.3 %collective-permute-start.1 = (bf16[2,4,128,128]{3,2,1,0:T(8,128)(2,1)S(1)}, bf16[2,4,128,128]{3,2,1,0:T(8,128)(2,1)S(1)}, u32[]{:S(2)}, u32[]{:S(2)}) collective-permute-start(bf16[2,4,128,128]{3,2,1,0:T(8,128)(2,1)S(1)} %get-tuple-element.13), channel_id=1, source_target_pairs={{0,2},{1,3},{2,0},{3,1},{4,6},{5,7},{6,4},{7,5},{8,10},{9,11},{10,... | collective-permute-start | bytes 786440 | tf_op jit(solution)/shard_map/ppermute | solution.py:208
where the time goes:
time: 167 us; the launch traced here: 166 us
  waiting for transfers between devices  90.2 us (54%)
  starting transfers between devices  32.9 us (20%)
  Pallas kernels  31 us (19%)
  local copies, waits for them, and re-layouts  11.3 us (7%)
    all_to_all x2, waiting for transfers between devices, on_device(): lax.all_to_all(piece, 'pencil', split_axis=0, concat_axis=0, tiled=True)  78.5 us
    all_to_all x2, starting transfers between devices, on_device(): lax.all_to_all(piece, 'pencil', split_axis=0, concat_axis=0, tiled=True)  22.8 us
    pallas_call x2, Pallas kernels, on_device(): pl.pallas_call(along_x, grid=(angles,), in_specs=[pl.BlockSpec((1, rows,...  14.5 us
    ppermute x2, waiting for transfers between devices, on_device(): joined += [keep, lax.ppermute(send, 'angle', FAR)]  11.7 us
    unnamed x26, local copies, waits for them, and re-layouts  11.3 us
    pallas_call x1, Pallas kernels, on_device(): pl.pallas_call(along_z, grid=(size_x // block,), in_specs=[pl.BlockSpec((...  8.09 us
    ppermute x2, starting transfers between devices, on_device(): other = lax.ppermute(send, 'angle', CORE)  6.99 us
    pallas_call x2, Pallas kernels, on_device(): pl.pallas_call(lambda *refs: along_y(*refs, scale=scale), grid=(count //...  5.96 us
  transfers between devices with their start and end apart: 6, of which 4 were waited for; matrix products, arithmetic and copies ran while one was open for 0% of the time, Pallas kernels for 9%

commit v1 on v0

v1 whole, which is shorter than its diff:
```python
import math

import jax
import jax.numpy as jnp
import numpy as np
from jax import lax
from jax.experimental import pallas as pl
from jax.experimental.pallas import tpu as pltpu
from jax.sharding import PartitionSpec as P

CHUNKS = (6, 2)
CORE = ((0, 1), (1, 0), (2, 3), (3, 2))
FAR = ((0, 2), (1, 3), (2, 0), (3, 1))


def phases(length):
    k = np.arange(length, dtype=np.int64)
    angle = (k[:, None] * k[None, :] % length) * (2.0 * math.pi / length)
    return np.cos(angle), np.sin(angle)


def z_table(size_z):
    cos, sin = phases(size_z)
    return np.block([[cos, sin], [-sin, cos]]).astype(jnp.bfloat16)


def x_table(size_x, groups, first, count):
    cos, sin = phases(size_x)
    each = size_x // groups
    rows = (np.arange(groups)[:, None] * each + np.arange(first, first + count)[None, :]).reshape(-1)
    return np.concatenate([cos[rows], sin[rows]], 0).astype(jnp.bfloat16)


def y_table(size_y, groups):
    cos, sin = phases(size_y)
    both = np.stack([cos.reshape(size_y, groups, -1), -sin.reshape(size_y, groups, -1)], 2)
    return both.reshape(size_y, -1).astype(jnp.bfloat16)


def spin(q, table, tmp, put, unroll):
    rows, _, width = q.shape
    size_z = width // 2
    half = table.shape[0] // 2

    def one(k, carry):
        both = jnp.dot(table[...], q[k], preferred_element_type=jnp.float32)
        tmp[0, pl.ds(k, half, stride=rows), :] = both[:half, :size_z] - both[half:, size_z:]
        tmp[1, pl.ds(k, half, stride=rows), :] = both[half:, :size_z] + both[:half, size_z:]
        return carry

    lax.fori_loop(0, rows, one, 0, unroll=unroll)
    pair = [tmp[h].reshape(half, rows, size_z) for h in range(2)]
    put(jnp.concatenate(pair, 1).astype(jnp.bfloat16))


def front(tr, ti, ar, ai, flags, z_tab, x_tab, q_out, sent_out, *scratch):
    btr, bti, bar, bai, bfl, bz, bx, tmp, q, wide, sent, sems, more = scratch
    angles, size_x, rows, size_z = bar.shape
    blocks = sems.shape[0]
    block = size_x // blocks

    def copies(b):
        at = pl.ds(pl.multiple_of(b * block, block), block)
        pairs = [(tr.at[at], btr.at[at]), (ti.at[at], bti.at[at]), (flags.at[at], bfl.at[at])]
        pairs += [(ar.at[:, at], bar.at[:, at]), (ai.at[:, at], bai.at[:, at])]
        return [pltpu.make_async_copy(s, d, sems.at[b, j]) for j, (s, d) in enumerate(pairs)]

    def begin(b, carry):
        for c in copies(b):
            c.start()
        return carry

    tables = [
        pltpu.make_async_copy(z_tab, bz, more.at[0]),
        pltpu.make_async_copy(x_tab, bx, more.at[1]),
    ]
    tables[0].start()
    lax.fori_loop(0, blocks, begin, 0)
    tables[1].start()
    tables[0].wait()

    def one(b, carry):
        for c in copies(b):
            c.wait()
        first = pl.multiple_of(b * block, block)
        at = pl.ds(first, block)
        flag = bfl[at].astype(jnp.float32)
        fr = btr[at].astype(jnp.float32) * flag
        fi = bti[at].astype(jnp.float32) * flag
        for a in range(angles):
            br = bar[a, at].astype(jnp.float32)
            bi = bai[a, at].astype(jnp.float32)
            pr = (fr * br + fi * bi).astype(jnp.bfloat16).reshape(block * rows, size_z)
            pi = (fi * br - fr * bi).astype(jnp.bfloat16).reshape(block * rows, size_z)
            both = jnp.concatenate([pr, pi], 1)
            sums = jnp.dot(both, bz[...], preferred_element_type=jnp.float32)
            tmp[2 * a] = sums[:, :size_z]
            tmp[2 * a + 1] = sums[:, size_z:]
            for k in range(rows):
                half = [tmp[2 * a + h, pl.ds(k, block, stride=rows), :] for h in range(2)]
                q[a, k, at, :] = jnp.concatenate(half, 1).astype(jnp.bfloat16)
        return carry

    lax.fori_loop(0, blocks, one, 0)
    leaving = [pltpu.make_async_copy(q, q_out, more.at[2])]
    leaving[0].start()
    tables[1].wait()
    for a in range(angles):

        def put(value, a=a):
            sent[a] = value.reshape(sent.shape[1:])

        spin(q.at[a], bx, wide, put, 4)
        leaving.append(pltpu.make_async_copy(sent.at[a], sent_out.at[:, a], more.at[3 + a]))
        leaving[-1].start()
    for c in leaving:
        c.wait()


def along_x(q, table, out, tmp):
    def put(value):
        out[...] = value.reshape(out.shape)

    spin(q.at[0], table, tmp, put, 2)


def along_y(who, got, sigma, table, keep, send, *, scale):
    groups, angles, count, pair, size_z = got.shape
    me = who[0]
    part = table.shape[0] // 4
    starts = [pl.multiple_of(jnp.bitwise_xor(me, r) * part, part) for r in range(4)]
    left = jnp.concatenate([table[pl.ds(s, part), :] for s in starts], 0)
    sums = []
    for a in range(angles):
        right = jnp.concatenate([got[:, a, i].reshape(groups * pair, size_z) for i in range(count)], 1)
        sums.append(jnp.dot(left, right, preferred_element_type=jnp.float32))
    for i in range(count):
        for r in range(4):
            here = (slice(r * part, (r + 1) * part), slice(i * size_z, (i + 1) * size_z))
            inverse = scale / sigma[i, pl.ds(starts[r], part), :]
            best = sums[0][here] * inverse
            runner = jnp.full_like(best, -1e30)
            for a in range(1, angles):
                score = sums[a][here] * inverse
                runner = jnp.maximum(runner, jnp.minimum(best, score))
                best = jnp.maximum(best, score)
            to = send if r % 2 else keep
            to[r // 2, 0, i] = best.astype(jnp.bfloat16)
            to[r // 2, 1, i] = runner.astype(jnp.bfloat16)


def top_two(first, later):
    best = jnp.maximum(first[0], later[0])
    return best, jnp.maximum(jnp.minimum(first[0], later[0]), jnp.maximum(first[1], later[1]))


def join_core(mine, other, keep, send):
    for slot, to in enumerate((keep, send)):
        best, runner = top_two((mine[slot, 0], mine[slot, 1]), (other[slot, 0], other[slot, 1]))
        to[0] = best
        to[1] = runner


def join_far(mine, other, *outs):
    best, runner = top_two((mine[0], mine[1]), (other[0], other[1]))
    outs[-2][...] = best.astype(jnp.float32)
    outs[-1][...] = runner.astype(jnp.float32)


def cost(flops, moved):
    return pl.CostEstimate(flops=flops, bytes_accessed=moved, transcendentals=0)


def on_device(tomo_real, tomo_imag, template_real, template_imag, wedge_flags, local_sigma):
    size_x, rows, size_z = tomo_real.shape
    angles = template_real.shape[0]
    size_y = local_sigma.shape[1]
    groups = size_y // rows
    part = size_y // 4
    scale = 1.0 / math.sqrt(size_x * size_y * size_z)
    block = 64
    params = pltpu.CompilerParams(vmem_limit_bytes=48 * 1024 * 1024)

    anywhere = pl.BlockSpec(memory_space=pl.ANY)
    blocks = size_x // block
    vmem = pltpu.VMEM
    count = CHUNKS[0]
    table = x_table(size_x, groups, 0, count)
    whole = (size_x, rows, size_z)
    spectrum, piece = pl.pallas_call(
        front,
        in_specs=[anywhere] * 7,
        out_specs=[anywhere] * 2,
        out_shape=[
            jax.ShapeDtypeStruct((angles, rows, size_x, 2 * size_z), jnp.bfloat16),
            jax.ShapeDtypeStruct((groups, angles, count, 2 * rows, size_z), jnp.bfloat16),
        ],
        scratch_shapes=[
            vmem(whole, jnp.bfloat16),
            vmem(whole, jnp.bfloat16),
            vmem((angles,) + whole, jnp.bfloat16),
            vmem((angles,) + whole, jnp.bfloat16),
            vmem(whole, jnp.int32),
            vmem((2 * size_z, 2 * size_z), jnp.bfloat16),
            vmem(table.shape, jnp.bfloat16),
            vmem((2 * angles, block * rows, size_z), jnp.float32),
            vmem((angles, rows, size_x, 2 * size_z), jnp.bfloat16),
            vmem((2, groups * count * rows, size_z), jnp.float32),
            vmem((angles, groups, count, 2 * rows, size_z), jnp.bfloat16),
            pltpu.SemaphoreType.DMA((blocks, 5)),
            pltpu.SemaphoreType.DMA((3 + angles,)),
        ],
        compiler_params=pltpu.CompilerParams(vmem_limit_bytes=60 * 1024 * 1024),
        cost_estimate=cost(8 * angles * size_x * rows * size_z * size_z, 12 * 2**20),
        name="front",
    )(tomo_real, tomo_imag, template_real, template_imag, wedge_flags, z_table(size_z), table)

    me = lax.axis_index("angle").astype(jnp.int32)[None]
    columns = y_table(size_y, groups)
    first = 0
    results = ()
    for at, count in enumerate(CHUNKS):
        if at:
            table = x_table(size_x, groups, first, count)
            piece = pl.pallas_call(
                along_x,
                grid=(angles,),
                in_specs=[
                    pl.BlockSpec((1, rows, size_x, 2 * size_z), lambda a: (a, 0, 0, 0)),
                    pl.BlockSpec(table.shape, lambda a: (0, 0)),
                ],
                out_specs=pl.BlockSpec((groups, 1, count, 2 * rows, size_z), lambda a: (0, a, 0, 0, 0)),
                out_shape=jax.ShapeDtypeStruct((groups, angles, count, 2 * rows, size_z), jnp.bfloat16),
                scratch_shapes=[vmem((2, groups * count * rows, size_z), jnp.float32)],
                compiler_params=params,
                cost_estimate=cost(8 * angles * size_x * groups * count * rows * size_z, 8 * 2**20),
                name="along_x",
            )(spectrum, table)
        got = lax.all_to_all(piece, "pencil", split_axis=0, concat_axis=0, tiled=True)
        step = 2 if count % 2 == 0 and first % 2 == 0 else 1
        out = jax.ShapeDtypeStruct((2, 2, count, part, size_z), jnp.bfloat16)
        keep, send = pl.pallas_call(
            lambda *refs: along_y(*refs, scale=scale),
            grid=(count // step,),
            in_specs=[
                pl.BlockSpec(memory_space=pltpu.SMEM),
                pl.BlockSpec((groups, angles, step, 2 * rows, size_z), lambda i: (0, 0, i, 0, 0)),
                pl.BlockSpec((step, size_y, size_z), lambda i, o=first // step: (i + o, 0, 0)),
                pl.BlockSpec(columns.shape, lambda i: (0, 0)),
            ],
            out_specs=[pl.BlockSpec((2, 2, step, part, size_z), lambda i: (0, 0, i, 0, 0))] * 2,
            out_shape=[out, out],
            compiler_params=params,
            cost_estimate=cost(4 * angles * count * size_y * size_y * size_z, 2 * 2**20 * count),
            name="along_y",
        )(me, got, local_sigma, columns)
        other = lax.ppermute(send, "angle", CORE)
        near = jax.ShapeDtypeStruct((2, count, part, size_z), jnp.bfloat16)
        keep, send = pl.pallas_call(
            join_core,
            out_shape=[near, near],
            compiler_params=params,
            cost_estimate=cost(2**20 * count, 2**19 * count),
            name="join_core",
        )(keep, other)
        other = lax.ppermute(send, "angle", FAR)
        done = jax.ShapeDtypeStruct((local_sigma.shape[0], part, size_z), jnp.float32)
        narrow = pl.BlockSpec((2, step, part, size_z), lambda i: (0, i, 0, 0))
        results = pl.pallas_call(
            join_far,
            grid=(count // step,),
            in_specs=[narrow, narrow] + [anywhere] * len(results),
            out_specs=[pl.BlockSpec((step, part, size_z), lambda i, o=first // step: (i + o, 0, 0))] * 2,
            out_shape=[done, done],
            input_output_aliases={2: 0, 3: 1} if results else {},
            compiler_params=params,
            cost_estimate=cost(2**20, 2**21),
            name="join_far",
        )(keep, other, *results)
        first += count
    return tuple(results)


def solution(mesh):
    in_specs = (
        P(None, "pencil", None),
        P(None, "pencil", None),
        P("angle", None, "pencil", None),
        P("angle", None, "pencil", None),
        P(None, "pencil", None),
        P("pencil", None, None),
    )
    out_specs = (P("pencil", "angle", None), P("pencil", "angle", None))
    return jax.shard_map(on_device, mesh=mesh, in_specs=in_specs, out_specs=out_specs, check_vma=False)
```

time: 167 us -> 155 us (0.928)
  local copies, waits for them, and re-layouts: 11.3 us -> 4.06 us
  Pallas kernels: 31 us -> 24.2 us
  waiting for transfers between devices: 90.2 us -> 92.7 us
    pallas_call x2 -> x1, Pallas kernels: 14.5 us -> 2.75 us  [on_device(): pl.pallas_call(along_x, grid=(angles,), in_specs=[pl.BlockSpec((1, rows,...]
    unnamed x26 -> x14, local copies, waits for them, and re-layouts: 11.3 us -> 4.06 us
    pallas_call x2 -> x3, Pallas kernels: 9.2 us -> 13.2 us  [the longest x1 10.9 us: on_device(): pl.pallas_call(front, in_specs=[anywhere] * 7, out_specs=[anywhere] * 2,...]
    all_to_all x2, waiting for transfers between devices: 78.5 us -> 82.4 us  [on_device(): lax.all_to_all(piece, 'pencil', split_axis=0, concat_axis=0, tiled=True)]
    all_to_all x2, starting transfers between devices: 22.8 us -> 24.9 us  [on_device(): lax.all_to_all(piece, 'pencil', split_axis=0, concat_axis=0, tiled=True)]
    ppermute x2, starting transfers between devices: 6.99 us -> 4.9 us  [on_device(): other = lax.ppermute(send, 'angle', CORE)]
  transfers between devices with their start and end apart: 6 -> 6, of which waited for: 4 -> 4; matrix products, arithmetic and copies ran while one was open for 0% -> 0% of each run, Pallas kernels for 9% -> 8%
where the time goes in v1:
time: 155 us
  waiting for transfers between devices  92.7 us (60%)
  starting transfers between devices  32.9 us (21%)
  Pallas kernels  24.2 us (16%)
  local copies, waits for them, and re-layouts  4.06 us (3%)
    all_to_all x2, waiting for transfers between devices, on_device(): lax.all_to_all(piece, 'pencil', split_axis=0, concat_axis=0, tiled=True)  82.4 us
    all_to_all x2, starting transfers between devices, on_device(): lax.all_to_all(piece, 'pencil', split_axis=0, concat_axis=0, tiled=True)  24.9 us
    pallas_call x1, Pallas kernels, on_device(): pl.pallas_call(front, in_specs=[anywhere] * 7, out_specs=[anywhere] * 2,...  10.9 us
    ppermute x2, waiting for transfers between devices, on_device(): other = lax.ppermute(send, 'angle', FAR)  10.3 us
    pallas_call x2, Pallas kernels, on_device(): pl.pallas_call(lambda *refs: along_y(*refs, scale=scale), grid=(count //...  6.79 us
    ppermute x2, starting transfers between devices, on_device(): other = lax.ppermute(send, 'angle', CORE)  4.9 us
    unnamed x14, local copies, waits for them, and re-layouts  4.06 us
    ppermute x2, starting transfers between devices, on_device(): other = lax.ppermute(send, 'angle', FAR)  3.14 us
  transfers between devices with their start and end apart: 6, of which 4 were waited for; matrix products, arithmetic and copies ran while one was open for 0% of the time, Pallas kernels for 8%

profile of v1, /device:TPU:1, one launch (start us, length us, event | category | flops | bytes accessed | tf_op | source)
XLA Modules:
  0.0 154.6 jit_solution(3585247822113971894)
XLA Ops:
  0.6 10.9 %front.1 = (bf16[2,8,512,256]{3,2,1,0:T(8,128)(2,1)}, bf16[64,2,6,16,128]{4,3,2,1,0:T(8,128)(2,1)}) custom-call(bf16[512,8,128]{2,1,0:T(8,128)(2,1)} %tr.1, bf16[512,8,128]{2,1,0:T(8,128)(2,1)} %ti.1, bf16[2,512,8,128]{3,2,1,0:T(8,128)(2,1)} %ar.1, bf16[2,512,8,128]{3,2,1,0:T(8,128)(2,1)} %ai.1, s32[512,8,128]{2,1,0:T(8,128)} %flags.1, ...), custom_call_target="tpu_custom_call" | custom-call | flops 1073741824 | bytes 12582912 | tf_op jit(solution)/shard_map/front/pallas_call | solution.py:190
  11.6 0.0 copy-start.6
  11.6 13.9 %all-to-all-start.1 = ((bf16[64,2,6,16,128]{4,3,2,1,0:T(8,128)(2,1)}), bf16[64,2,6,16,128]{4,3,2,1,0:T(8,128)(2,1)}, u32[]{:S(2)}, u32[]{:S(2)}) async-start(bf16[64,2,6,16,128]{4,3,2,1,0:T(8,128)(2,1)} %get-tuple-element.19), calls=%async_computation.1 | async-start | bytes 6291456 | tf_op jit(solution)/shard_map/all_to_all | solution.py:239
  25.5 0.0 copy-done.6
  25.6 0.0 copy-start.2
  25.6 2.2 %copy-done.2 = bf16[2,8,512,256]{3,2,1,0:T(8,128)(2,1)S(1)} copy-done((bf16[2,8,512,256]{3,2,1,0:T(8,128)(2,1)S(1)}, bf16[2,8,512,256]{3,2,1,0:T(8,128)(2,1)}, u32[]{:S(2)}) %copy-start.2) | copy-done | bytes 4194328
  27.7 0.0 copy-start.1
  27.7 2.8 %along_x.1 = bf16[64,2,2,16,128]{4,3,2,1,0:T(8,128)(2,1)S(1)} custom-call(bf16[2,8,512,256]{3,2,1,0:T(8,128)(2,1)S(1)} %copy-done.2, bf16[256,512]{1,0:T(8,128)(2,1)S(1)} %copy-done.6), custom_call_target="tpu_custom_call" | custom-call | flops 1073741824 | bytes 8388608 | tf_op jit(solution)/shard_map/along_x/pallas_call | solution.py:225
  30.5 0.0 copy-start.3
  30.5 1.0 copy-done.3
  31.5 0.0 copy-start
  31.5 63.0 %all-to-all-done.1.refs_1_ = bf16[64,2,6,16,128]{4,3,2,1,0:T(8,128)(2,1)} async-done(((bf16[64,2,6,16,128]{4,3,2,1,0:T(8,128)(2,1)}), bf16[64,2,6,16,128]{4,3,2,1,0:T(8,128)(2,1)}, u32[]{:S(2)}, u32[]{:S(2)}) %all-to-all-start.1) | async-done | bytes 3145760 | tf_op jit(solution)/shard_map/all_to_all | solution.py:239
  94.5 10.9 %all-to-all-start = ((bf16[64,2,2,16,128]{4,3,2,1,0:T(8,128)(2,1)}), bf16[64,2,2,16,128]{4,3,2,1,0:T(8,128)(2,1)}, u32[]{:S(2)}, u32[]{:S(2)}) async-start(bf16[64,2,2,16,128]{4,3,2,1,0:T(8,128)(2,1)} %copy-done.3), calls=%async_computation | async-start | bytes 2097152 | tf_op jit(solution)/shard_map/all_to_all | solution.py:239
  105.4 0.0 copy-done.1
  105.4 0.0 copy-done
  105.4 4.8 %along_y.3 = (bf16[2,2,6,128,128]{4,3,2,1,0:T(8,128)(2,1)S(1)}, bf16[2,2,6,128,128]{4,3,2,1,0:T(8,128)(2,1)}) custom-call(s32[1]{0:T(128)} %bitcast.refs_0_, bf16[64,2,6,16,128]{4,3,2,1,0:T(8,128)(2,1)} %all-to-all-done.1.refs_1_, f32[8,512,128]{2,1,0:T(8,128)S(1)} %copy-done, bf16[512,1024]{1,0:T(8,128)(2,1)S(1)} %copy-done.1), custom_call_target="tpu_custom_call" | custom-call | flops 1610612736 | bytes 12582912 | tf_op jit(solution)/shard_map/along_y/pallas_call | solution.py:242
  110.2 0.0 copy-start.4
  110.2 0.9 copy-done.4
  111.1 1.2 collective-permute-start.2
  112.3 19.4 %all-to-all-done.refs_1_ = bf16[64,2,2,16,128]{4,3,2,1,0:T(8,128)(2,1)} async-done(((bf16[64,2,2,16,128]{4,3,2,1,0:T(8,128)(2,1)}), bf16[64,2,2,16,128]{4,3,2,1,0:T(8,128)(2,1)}, u32[]{:S(2)}, u32[]{:S(2)}) %all-to-all-start) | async-done | bytes 1048608 | tf_op jit(solution)/shard_map/all_to_all | solution.py:239
  131.7 0.0 copy-start.5
  131.7 2.0 %along_y.2 = (bf16[2,2,2,128,128]{4,3,2,1,0:T(8,128)(2,1)S(1)}, bf16[2,2,2,128,128]{4,3,2,1,0:T(8,128)(2,1)S(1)}) custom-call(s32[1]{0:T(128)} %bitcast.refs_0_, bf16[64,2,2,16,128]{4,3,2,1,0:T(8,128)(2,1)} %all-to-all-done.refs_1_, f32[8,512,128]{2,1,0:T(8,128)S(1)} %copy-done, bf16[512,1024]{1,0:T(8,128)(2,1)S(1)} %copy-done.1), custom_call_target="tpu_custom_call" | custom-call | flops 536870912 | bytes 4194304 | tf_op jit(solution)/shard_map/along_y/pallas_call | solution.py:242
  133.7 3.7 %collective-permute-start = (bf16[2,2,2,128,128]{4,3,2,1,0:T(8,128)(2,1)S(1)}, bf16[2,2,2,128,128]{4,3,2,1,0:T(8,128)(2,1)S(1)}, u32[]{:S(2)}, u32[]{:S(2)}) collective-permute-start(bf16[2,2,2,128,128]{4,3,2,1,0:T(8,128)(2,1)S(1)} %get-tuple-element.16), channel_id=1, source_target_pairs={{0,1},{1,0},{2,3},{3,2},{4,5},{5,4},{6,7},{7,6},{8,9},{9,8},{10,11... | collective-permute-start | bytes 786440 | tf_op jit(solution)/shard_map/ppermute | solution.py:257
  137.4 0.0 collective-permute-done.2.other
  137.4 0.0 copy-done.5
  137.4 1.4 join_core.3
  138.8 2.5 %collective-permute-start.3 = (bf16[2,6,128,128]{3,2,1,0:T(8,128)(2,1)S(1)}, bf16[2,6,128,128]{3,2,1,0:T(8,128)(2,1)S(1)}, u32[]{:S(2)}, u32[]{:S(2)}) collective-permute-start(bf16[2,6,128,128]{3,2,1,0:T(8,128)(2,1)S(1)} %get-tuple-element.23), channel_id=1, source_target_pairs={{0,2},{1,3},{2,0},{3,1},{4,6},{5,7},{6,4},{7,5},{8,10},{9,11},{10,... | collective-permute-start | bytes 1179656 | tf_op jit(solution)/shard_map/ppermute | solution.py:266
  141.3 0.0 collective-permute-done.other
  141.3 0.1 join_core.2
  141.4 0.6 collective-permute-start.1
  142.0 9.0 %collective-permute-done.3.other = bf16[2,6,128,128]{3,2,1,0:T(8,128)(2,1)S(1)} collective-permute-done((bf16[2,6,128,128]{3,2,1,0:T(8,128)(2,1)S(1)}, bf16[2,6,128,128]{3,2,1,0:T(8,128)(2,1)S(1)}, u32[]{:S(2)}, u32[]{:S(2)}) %collective-permute-start.3) | collective-permute-done | bytes 393248 | tf_op jit(solution)/shard_map/ppermute | solution.py:266
  151.0 1.5 join_far.2
  152.5 1.3 collective-permute-done.1.other
  153.8 0.7 join_far.3
Async XLA Ops:
  11.6 14.0 %copy-start.6 = (bf16[256,512]{1,0:T(8,128)(2,1)S(1)}, bf16[256,512]{1,0:T(8,128)(2,1)}, u32[]{:S(2)}) copy-start(bf16[256,512]{1,0:T(8,128)(2,1)} %constant.15.clone.table) | copy-start | bytes 786436
  11.6 82.9 %all-to-all-start.1 = ((bf16[64,2,6,16,128]{4,3,2,1,0:T(8,128)(2,1)}), bf16[64,2,6,16,128]{4,3,2,1,0:T(8,128)(2,1)}, u32[]{:S(2)}, u32[]{:S(2)}) async-start(bf16[64,2,6,16,128]{4,3,2,1,0:T(8,128)(2,1)} %get-tuple-element.19), calls=%async_computation.1 | async-start | bytes 6291456 | tf_op jit(solution)/shard_map/all_to_all | solution.py:239
  25.6 2.2 %copy-start.2 = (bf16[2,8,512,256]{3,2,1,0:T(8,128)(2,1)S(1)}, bf16[2,8,512,256]{3,2,1,0:T(8,128)(2,1)}, u32[]{:S(2)}) copy-start(bf16[2,8,512,256]{3,2,1,0:T(8,128)(2,1)} %get-tuple-element.14.q) | copy-start | bytes 12582916
  27.7 77.7 %copy-start.1 = (bf16[512,1024]{1,0:T(8,128)(2,1)S(1)}, bf16[512,1024]{1,0:T(8,128)(2,1)}, u32[]{:S(2)}) copy-start(bf16[512,1024]{1,0:T(8,128)(2,1)} %constant.14.clone.refs_3_) | copy-start | bytes 3145732
  30.5 1.0 copy-start.3
  31.5 73.9 %copy-start = (f32[8,512,128]{2,1,0:T(8,128)S(1)}, f32[8,512,128]{2,1,0:T(8,128)}, u32[]{:S(2)}) copy-start(f32[8,512,128]{2,1,0:T(8,128)} %refs_2_.3) | copy-start | bytes 6291460
  94.5 37.2 %all-to-all-start = ((bf16[64,2,2,16,128]{4,3,2,1,0:T(8,128)(2,1)}), bf16[64,2,2,16,128]{4,3,2,1,0:T(8,128)(2,1)}, u32[]{:S(2)}, u32[]{:S(2)}) async-start(bf16[64,2,2,16,128]{4,3,2,1,0:T(8,128)(2,1)} %copy-done.3), calls=%async_computation | async-start | bytes 2097152 | tf_op jit(solution)/shard_map/all_to_all | solution.py:239
  110.2 0.9 copy-start.4
  111.1 26.3 %collective-permute-start.2 = (bf16[2,2,6,128,128]{4,3,2,1,0:T(8,128)(2,1)}, bf16[2,2,6,128,128]{4,3,2,1,0:T(8,128)(2,1)}, u32[]{:S(2)}, u32[]{:S(2)}) collective-permute-start(bf16[2,2,6,128,128]{4,3,2,1,0:T(8,128)(2,1)} %get-tuple-element.21), channel_id=1, source_target_pairs={{0,1},{1,0},{2,3},{3,2},{4,5},{5,4},{6,7},{7,6},{8,9},{9,8},{10,11... | collective-permute-start | bytes 2359304 | tf_op jit(solution)/shard_map/ppermute | solution.py:257
  131.7 5.7 %copy-start.5 = (bf16[2,2,6,128,128]{4,3,2,1,0:T(8,128)(2,1)S(1)}, bf16[2,2,6,128,128]{4,3,2,1,0:T(8,128)(2,1)}, u32[]{:S(2)}) copy-start(bf16[2,2,6,128,128]{4,3,2,1,0:T(8,128)(2,1)} %copy-done.4) | copy-start | bytes 2359300
  133.7 7.6 %collective-permute-start = (bf16[2,2,2,128,128]{4,3,2,1,0:T(8,128)(2,1)S(1)}, bf16[2,2,2,128,128]{4,3,2,1,0:T(8,128)(2,1)S(1)}, u32[]{:S(2)}, u32[]{:S(2)}) collective-permute-start(bf16[2,2,2,128,128]{4,3,2,1,0:T(8,128)(2,1)S(1)} %get-tuple-element.16), channel_id=1, source_target_pairs={{0,1},{1,0},{2,3},{3,2},{4,5},{5,4},{6,7},{7,6},{8,9},{9,8},{10,11... | collective-permute-start | bytes 786440 | tf_op jit(solution)/shard_map/ppermute | solution.py:257
  138.8 12.2 %collective-permute-start.3 = (bf16[2,6,128,128]{3,2,1,0:T(8,128)(2,1)S(1)}, bf16[2,6,128,128]{3,2,1,0:T(8,128)(2,1)S(1)}, u32[]{:S(2)}, u32[]{:S(2)}) collective-permute-start(bf16[2,6,128,128]{3,2,1,0:T(8,128)(2,1)S(1)} %get-tuple-element.23), channel_id=1, source_target_pairs={{0,2},{1,3},{2,0},{3,1},{4,6},{5,7},{6,4},{7,5},{8,10},{9,11},{10,... | collective-permute-start | bytes 1179656 | tf_op jit(solution)/shard_map/ppermute | solution.py:266
  141.4 12.4 %collective-permute-start.1 = (bf16[2,2,128,128]{3,2,1,0:T(8,128)(2,1)S(1)}, bf16[2,2,128,128]{3,2,1,0:T(8,128)(2,1)S(1)}, u32[]{:S(2)}, u32[]{:S(2)}) collective-permute-start(bf16[2,2,128,128]{3,2,1,0:T(8,128)(2,1)S(1)} %get-tuple-element.18), channel_id=1, source_target_pairs={{0,2},{1,3},{2,0},{3,1},{4,6},{5,7},{6,4},{7,5},{8,10},{9,11},{10,... | collective-permute-start | bytes 393224 | tf_op jit(solution)/shard_map/ppermute | solution.py:266

commit v2 on v1

--- a/solution.py
+++ b/solution.py
@@ -11,6 +11,19 @@
 CHUNKS = (6, 2)
 CORE = ((0, 1), (1, 0), (2, 3), (3, 2))
 FAR = ((0, 2), (1, 3), (2, 0), (3, 1))
+SIDES = (4, 2, 8)
+NEAR = tuple((dy, dx) for dy in range(SIDES[0]) for dx in range(SIDES[1]))
+
+
+def place(at, dy, dx, dz):
+    _, sx, sz = SIDES
+    y = (at // (sx * sz) + dy) % SIDES[0]
+    x = (at // sz + dx) % sx
+    return (y * sx + x) * sz + (at + dz) % sz
+
+
+def hop(dy, dx, dz):
+    return tuple((p, place(p, dy, dx, dz)) for p in range(math.prod(SIDES)))
 
 
 def phases(length):
@@ -21,7 +34,7 @@
 
 def z_table(size_z):
     cos, sin = phases(size_z)
-    return np.block([[cos, sin], [-sin, cos]]).astype(jnp.bfloat16)
+    return np.concatenate([cos, sin], 1).astype(jnp.bfloat16)
 
 
 def x_table(size_x, groups, first, count):
@@ -37,7 +50,7 @@
     return both.reshape(size_y, -1).astype(jnp.bfloat16)
 
 
-def spin(q, table, tmp, put, unroll):
+def spin(q, table, tmp, unroll):
     rows, _, width = q.shape
     size_z = width // 2
     half = table.shape[0] // 2
@@ -49,8 +62,6 @@
         return carry
 
     lax.fori_loop(0, rows, one, 0, unroll=unroll)
-    pair = [tmp[h].reshape(half, rows, size_z) for h in range(2)]
-    put(jnp.concatenate(pair, 1).astype(jnp.bfloat16))
 
 
 def front(tr, ti, ar, ai, flags, z_tab, x_tab, q_out, sent_out, *scratch):
@@ -71,13 +82,15 @@
         return carry
 
     tables = [
-        pltpu.make_async_copy(z_tab, bz, more.at[0]),
+        pltpu.make_async_copy(z_tab, bz.at[pl.ds(0, size_z)], more.at[0]),
         pltpu.make_async_copy(x_tab, bx, more.at[1]),
     ]
     tables[0].start()
     lax.fori_loop(0, blocks, begin, 0)
     tables[1].start()
     tables[0].wait()
+    bz[size_z:, :size_z] = -bz[:size_z, size_z:]
+    bz[size_z:, size_z:] = bz[:size_z, :size_z]
 
     def one(b, carry):
         for c in copies(b):
@@ -106,25 +119,44 @@
     leaving[0].start()
     tables[1].wait()
     for a in range(angles):
-
-        def put(value, a=a):
-            sent[a] = value.reshape(sent.shape[1:])
-
-        spin(q.at[a], bx, wide, put, 4)
+        spin(q.at[a], bx, wide, 2)
+        pair = [wide[h].reshape(-1, rows, size_z) for h in range(2)]
+        sent[a] = jnp.concatenate(pair, 1).astype(jnp.bfloat16).reshape(sent.shape[1:])
         leaving.append(pltpu.make_async_copy(sent.at[a], sent_out.at[:, a], more.at[3 + a]))
         leaving[-1].start()
     for c in leaving:
         c.wait()
 
 
-def along_x(q, table, out, tmp):
-    def put(value):
-        out[...] = value.reshape(out.shape)
-
-    spin(q.at[0], table, tmp, put, 2)
-
-
-def along_y(who, got, sigma, table, keep, send, *, scale):
+def along_x(who, q, table, *rest):
+    outs, tmp = rest[:-1], rest[-1]
+    steps, _, count, pair, size_z = outs[0].shape
+    rows = pair // 2
+    each = count * rows
+    spin(q.at[0], table, tmp, 1)
+    for out, (dy, dx) in zip(outs, NEAR):
+        for dz in range(steps):
+            at = pl.ds(pl.multiple_of(place(who[0], dy, dx, dz) * each, each), each)
+            halves = [tmp[h, at, :].reshape(count, rows, size_z) for h in range(2)]
+            out[dz, 0] = jnp.concatenate(halves, 1).astype(jnp.bfloat16)
+
+
+def regroup(*refs):
+    half = len(refs) // 2
+    for dz, out in enumerate(refs[half:]):
+        for i, piece in enumerate(refs[:half]):
+            out[i] = piece[dz]
+
+
+def collect_along_y(who, me, *refs):
+    pieces, (inverse, table, keep, send, got) = refs[:-5], refs[-5:]
+    for dz, piece in enumerate(pieces):
+        for i, (dy, dx) in enumerate(NEAR):
+            got[place(me[0], SIDES[0] - dy, SIDES[1] - dx, SIDES[2] - dz)] = piece[i]
+    along_y(who, got, inverse, table, keep, send)
+
+
+def along_y(who, got, inverse, table, keep, send):
     groups, angles, count, pair, size_z = got.shape
     me = who[0]
     part = table.shape[0] // 4
@@ -137,16 +169,20 @@
     for i in range(count):
         for r in range(4):
             here = (slice(r * part, (r + 1) * part), slice(i * size_z, (i + 1) * size_z))
-            inverse = scale / sigma[i, pl.ds(starts[r], part), :]
-            best = sums[0][here] * inverse
+            factor = inverse[i, pl.ds(starts[r], part), :]
+            best = sums[0][here] * factor
             runner = jnp.full_like(best, -1e30)
             for a in range(1, angles):
-                score = sums[a][here] * inverse
+                score = sums[a][here] * factor
                 runner = jnp.maximum(runner, jnp.minimum(best, score))
                 best = jnp.maximum(best, score)
             to = send if r % 2 else keep
             to[r // 2, 0, i] = best.astype(jnp.bfloat16)
             to[r // 2, 1, i] = runner.astype(jnp.bfloat16)
+
+
+def invert(sigma, out, *, scale):
+    out[...] = scale / sigma[...]
 
 
 def top_two(first, later):
@@ -179,7 +215,8 @@
     part = size_y // 4
     scale = 1.0 / math.sqrt(size_x * size_y * size_z)
     block = 64
-    params = pltpu.CompilerParams(vmem_limit_bytes=48 * 1024 * 1024)
+    params = pltpu.CompilerParams(vmem_limit_bytes=20 * 1024 * 1024)
+    tight = pltpu.CompilerParams(vmem_limit_bytes=8 * 1024 * 1024)
 
     anywhere = pl.BlockSpec(memory_space=pl.ANY)
     blocks = size_x // block
@@ -216,69 +253,115 @@
     )(tomo_real, tomo_imag, template_real, template_imag, wedge_flags, z_table(size_z), table)
 
     me = lax.axis_index("angle").astype(jnp.int32)[None]
+    pencil = lax.axis_index("pencil").astype(jnp.int32)[None]
     columns = y_table(size_y, groups)
-    first = 0
-    results = ()
-    for at, count in enumerate(CHUNKS):
-        if at:
-            table = x_table(size_x, groups, first, count)
-            piece = pl.pallas_call(
-                along_x,
-                grid=(angles,),
-                in_specs=[
-                    pl.BlockSpec((1, rows, size_x, 2 * size_z), lambda a: (a, 0, 0, 0)),
-                    pl.BlockSpec(table.shape, lambda a: (0, 0)),
-                ],
-                out_specs=pl.BlockSpec((groups, 1, count, 2 * rows, size_z), lambda a: (0, a, 0, 0, 0)),
-                out_shape=jax.ShapeDtypeStruct((groups, angles, count, 2 * rows, size_z), jnp.bfloat16),
-                scratch_shapes=[vmem((2, groups * count * rows, size_z), jnp.float32)],
-                compiler_params=params,
-                cost_estimate=cost(8 * angles * size_x * groups * count * rows * size_z, 8 * 2**20),
-                name="along_x",
-            )(spectrum, table)
-        got = lax.all_to_all(piece, "pencil", split_axis=0, concat_axis=0, tiled=True)
-        step = 2 if count % 2 == 0 and first % 2 == 0 else 1
-        out = jax.ShapeDtypeStruct((2, 2, count, part, size_z), jnp.bfloat16)
-        keep, send = pl.pallas_call(
-            lambda *refs: along_y(*refs, scale=scale),
-            grid=(count // step,),
-            in_specs=[
-                pl.BlockSpec(memory_space=pltpu.SMEM),
-                pl.BlockSpec((groups, angles, step, 2 * rows, size_z), lambda i: (0, 0, i, 0, 0)),
-                pl.BlockSpec((step, size_y, size_z), lambda i, o=first // step: (i + o, 0, 0)),
-                pl.BlockSpec(columns.shape, lambda i: (0, 0)),
-            ],
-            out_specs=[pl.BlockSpec((2, 2, step, part, size_z), lambda i: (0, 0, i, 0, 0))] * 2,
-            out_shape=[out, out],
-            compiler_params=params,
-            cost_estimate=cost(4 * angles * count * size_y * size_y * size_z, 2 * 2**20 * count),
-            name="along_y",
-        )(me, got, local_sigma, columns)
+    scalar = pl.BlockSpec(memory_space=pltpu.SMEM)
+    first, count = CHUNKS
+    table = x_table(size_x, groups, first, count)
+    steps = SIDES[2]
+    bytes_out = 2 * groups * angles * count * 2 * rows * size_z
+
+    def block_of(shape):
+        return pl.BlockSpec(shape, lambda *_: (0,) * len(shape))
+
+    got = lax.all_to_all(piece, "pencil", split_axis=0, concat_axis=0, tiled=True)
+    pieces = pl.pallas_call(
+        along_x,
+        grid=(angles,),
+        in_specs=[scalar, pl.BlockSpec((1, rows, size_x, 2 * size_z), lambda a: (a, 0, 0, 0)), block_of(table.shape)],
+        out_specs=[pl.BlockSpec((steps, 1, count, 2 * rows, size_z), lambda a: (0, a, 0, 0, 0))]
+        * len(NEAR),
+        out_shape=[jax.ShapeDtypeStruct((steps, angles, count, 2 * rows, size_z), jnp.bfloat16)]
+        * len(NEAR),
+        scratch_shapes=[vmem((2, groups * count * rows, size_z), jnp.float32)],
+        compiler_params=params,
+        cost_estimate=cost(8 * angles * size_x * groups * count * rows * size_z, 8 * 2**20),
+        name="along_x",
+    )(pencil, spectrum, table)
+    moved = [pieces[0]]
+    for i in range(1, len(NEAR)):
+        moved.append(lax.ppermute(pieces[i], "pencil", hop(*NEAR[i], 0)))
+    pieces = pl.pallas_call(
+        regroup,
+        out_shape=[jax.ShapeDtypeStruct((len(NEAR), angles, count, 2 * rows, size_z), jnp.bfloat16)]
+        * steps,
+        compiler_params=tight,
+        cost_estimate=cost(2**20, 2 * bytes_out),
+        name="regroup",
+    )(*moved)
+    moved = [pieces[0]]
+    for dz in range(1, steps):
+        moved.append(lax.ppermute(pieces[dz], "pencil", hop(0, 0, dz)))
+    inverse = pl.pallas_call(
+        lambda *refs: invert(*refs, scale=scale),
+        grid=(4,),
+        in_specs=[pl.BlockSpec((local_sigma.shape[0] // 4, size_y, size_z), lambda i: (i, 0, 0))],
+        out_specs=pl.BlockSpec((local_sigma.shape[0] // 4, size_y, size_z), lambda i: (i, 0, 0)),
+        out_shape=jax.ShapeDtypeStruct(local_sigma.shape, jnp.float32),
+        compiler_params=tight,
+        cost_estimate=cost(2**20, 2**22),
+        name="invert",
+    )(local_sigma)
+
+    def join(first, count, step, keep, send, results):
         other = lax.ppermute(send, "angle", CORE)
         near = jax.ShapeDtypeStruct((2, count, part, size_z), jnp.bfloat16)
         keep, send = pl.pallas_call(
             join_core,
             out_shape=[near, near],
-            compiler_params=params,
+            compiler_params=tight,
             cost_estimate=cost(2**20 * count, 2**19 * count),
             name="join_core",
         )(keep, other)
         other = lax.ppermute(send, "angle", FAR)
         done = jax.ShapeDtypeStruct((local_sigma.shape[0], part, size_z), jnp.float32)
         narrow = pl.BlockSpec((2, step, part, size_z), lambda i: (0, i, 0, 0))
-        results = pl.pallas_call(
+        return pl.pallas_call(
             join_far,
             grid=(count // step,),
             in_specs=[narrow, narrow] + [anywhere] * len(results),
-            out_specs=[pl.BlockSpec((step, part, size_z), lambda i, o=first // step: (i + o, 0, 0))] * 2,
+            out_specs=[pl.BlockSpec((step, part, size_z), lambda i: (i + first // step, 0, 0))] * 2,
             out_shape=[done, done],
             input_output_aliases={2: 0, 3: 1} if results else {},
-            compiler_params=params,
+            compiler_params=tight,
             cost_estimate=cost(2**20, 2**21),
             name="join_far",
         )(keep, other, *results)
-        first += count
-    return tuple(results)
+
+    step = 2
+    out_block = pl.BlockSpec((2, 2, step, part, size_z), lambda i: (0, 0, i, 0, 0))
+    out = jax.ShapeDtypeStruct((2, 2, first, part, size_z), jnp.bfloat16)
+    keep, send = pl.pallas_call(
+        along_y,
+        grid=(first // step,),
+        in_specs=[
+            scalar,
+            pl.BlockSpec((groups, angles, step, 2 * rows, size_z), lambda i: (0, 0, i, 0, 0)),
+            pl.BlockSpec((step, size_y, size_z), lambda i: (i, 0, 0)),
+            block_of(columns.shape),
+        ],
+        out_specs=[out_block] * 2,
+        out_shape=[out, out],
+        compiler_params=params,
+        cost_estimate=cost(4 * angles * first * size_y * size_y * size_z, 2 * 2**20 * first),
+        name="along_y",
+    )(me, got, inverse, columns)
+    results = join(0, first, step, keep, send, ())
+    out = jax.ShapeDtypeStruct((2, 2, count, part, size_z), jnp.bfloat16)
+    keep, send = pl.pallas_call(
+        collect_along_y,
+        grid=(1,),
+        in_specs=[scalar, scalar]
+        + [block_of((len(NEAR), angles, count, 2 * rows, size_z))] * steps
+        + [pl.BlockSpec((step, size_y, size_z), lambda i: (first // step, 0, 0)), block_of(columns.shape)],
+        out_specs=[out_block] * 2,
+        out_shape=[out, out],
+        scratch_shapes=[vmem((groups, angles, count, 2 * rows, size_z), jnp.bfloat16)],
+        compiler_params=params,
+        cost_estimate=cost(4 * angles * count * size_y * size_y * size_z, 2 * 2**20 * count),
+        name="along_y",
+    )(me, pencil, *moved, inverse, columns)
+    return tuple(join(first, count, step, keep, send, results))
 
 
 def solution(mesh):

time: 155 us -> 192 us (1.24)
  waiting for transfers between devices: 92.7 us -> 118 us
  starting transfers between devices: 32.9 us -> 42.7 us
    ppermute x4 -> x18, waiting for transfers between devices: 10.3 us -> 50.7 us  [the longest x7 23.9 us: on_device(): moved.append(lax.ppermute(pieces[dz], 'pencil', hop(0, 0, dz)))]
    ppermute x4 -> x18, starting transfers between devices: 8.05 us -> 28.9 us  [the longest x2 12.5 us: join(): other = lax.ppermute(send, 'angle', CORE)]
    all_to_all x2 -> x1, waiting for transfers between devices: 82.4 us -> 67 us  [on_device(): lax.all_to_all(piece, 'pencil', split_axis=0, concat_axis=0, tiled=True)]
    all_to_all x2 -> x1, starting transfers between devices: 24.9 us -> 13.8 us  [on_device(): lax.all_to_all(piece, 'pencil', split_axis=0, concat_axis=0, tiled=True)]
    pallas_call x7 -> x9, Pallas kernels: 13.2 us -> 14.4 us  [the longest x1 4.81 us: on_device(): pl.pallas_call(along_y, grid=(first // step,), in_specs=[scalar, pl.Block...]
    unnamed x14 -> x12, local copies, waits for them, and re-layouts: 4.06 us -> 4.67 us
  transfers between devices with their start and end apart: 6 -> 19, of which waited for: 4 -> 10; matrix products, arithmetic and copies ran while one was open for 0% -> 0% of each run, Pallas kernels for 8% -> 5%
where the time goes in v2:
time: 192 us
  waiting for transfers between devices  118 us (61%)
  starting transfers between devices  42.7 us (22%)
  Pallas kernels  25.9 us (13%)
  local copies, waits for them, and re-layouts  4.67 us (2%)
    all_to_all x1, waiting for transfers between devices, on_device(): lax.all_to_all(piece, 'pencil', split_axis=0, concat_axis=0, tiled=True)  67 us
    ppermute x7, waiting for transfers between devices, on_device(): moved.append(lax.ppermute(pieces[dz], 'pencil', hop(0, 0, dz)))  23.9 us
    ppermute x7, waiting for transfers between devices, on_device(): moved.append(lax.ppermute(pieces[i], 'pencil', hop(*NEAR[i], 0)))  16.6 us
    all_to_all x1, starting transfers between devices, on_device(): lax.all_to_all(piece, 'pencil', split_axis=0, concat_axis=0, tiled=True)  13.8 us
    ppermute x2, starting transfers between devices, join(): other = lax.ppermute(send, 'angle', CORE)  12.5 us
    pallas_call x1, Pallas kernels, on_device(): pl.pallas_call(front, in_specs=[anywhere] * 7, out_specs=[anywhere] * 2,...  11.6 us
    ppermute x2, waiting for transfers between devices, join(): other = lax.ppermute(send, 'angle', FAR)  10.1 us
    ppermute x7, starting transfers between devices, on_device(): moved.append(lax.ppermute(pieces[dz], 'pencil', hop(0, 0, dz)))  7.94 us
  transfers between devices with their start and end apart: 19, of which 10 were waited for; matrix products, arithmetic and copies ran while one was open for 0% of the time, Pallas kernels for 5%

profile of v2, /device:TPU:1, one launch (start us, length us, event | category | flops | bytes accessed | tf_op | source)
XLA Modules:
  0.0 191.8 jit_solution(1316758462066214484)
XLA Ops:
  0.6 11.6 %front.1 = (bf16[2,8,512,256]{3,2,1,0:T(8,128)(2,1)}, bf16[64,2,6,16,128]{4,3,2,1,0:T(8,128)(2,1)}) custom-call(bf16[512,8,128]{2,1,0:T(8,128)(2,1)} %tr.1, bf16[512,8,128]{2,1,0:T(8,128)(2,1)} %ti.1, bf16[2,512,8,128]{3,2,1,0:T(8,128)(2,1)} %ar.1, bf16[2,512,8,128]{3,2,1,0:T(8,128)(2,1)} %ai.1, s32[512,8,128]{2,1,0:T(8,128)} %flags.1, ...), custom_call_target="tpu_custom_call" | custom-call | flops 1073741824 | bytes 12582912 | tf_op jit(solution)/shard_map/front/pallas_call | solution.py:227
  12.2 13.8 %all-to-all-start = ((bf16[64,2,6,16,128]{4,3,2,1,0:T(8,128)(2,1)}), bf16[64,2,6,16,128]{4,3,2,1,0:T(8,128)(2,1)}, u32[]{:S(2)}, u32[]{:S(2)}) async-start(bf16[64,2,6,16,128]{4,3,2,1,0:T(8,128)(2,1)} %get-tuple-element.51), calls=%async_computation | async-start | bytes 6291456 | tf_op jit(solution)/shard_map/all_to_all | solution.py:267
  26.0 0.0 copy-start.2
  26.1 1.6 copy-done.2
  27.6 0.3 invert.1.refs_8_.inverse
  28.0 67.0 %all-to-all-done.got = bf16[64,2,6,16,128]{4,3,2,1,0:T(8,128)(2,1)} async-done(((bf16[64,2,6,16,128]{4,3,2,1,0:T(8,128)(2,1)}), bf16[64,2,6,16,128]{4,3,2,1,0:T(8,128)(2,1)}, u32[]{:S(2)}, u32[]{:S(2)}) %all-to-all-start) | async-done | bytes 3145760 | tf_op jit(solution)/shard_map/all_to_all | solution.py:267
  95.0 4.8 %along_y.3 = (bf16[2,2,6,128,128]{4,3,2,1,0:T(8,128)(2,1)S(1)}, bf16[2,2,6,128,128]{4,3,2,1,0:T(8,128)(2,1)}) custom-call(s32[1]{0:T(128)} %bitcast.who, bf16[64,2,6,16,128]{4,3,2,1,0:T(8,128)(2,1)} %all-to-all-done.got, f32[8,512,128]{2,1,0:T(8,128)S(1)} %invert.1.refs_8_.inverse, bf16[512,1024]{1,0:T(8,128)(2,1)S(1)} %copy-done), custom_call_target="tpu_custom_call" | custom-call | flops 1610612736 | bytes 12582912 | tf_op jit(solution)/shard_map/along_y/pallas_call | solution.py:334
  99.8 0.9 copy-done.3
  100.7 6.3 %collective-permute-start.16 = (bf16[2,2,6,128,128]{4,3,2,1,0:T(8,128)(2,1)}, bf16[2,2,6,128,128]{4,3,2,1,0:T(8,128)(2,1)}, u32[]{:S(2)}, u32[]{:S(2)}) collective-permute-start(bf16[2,2,6,128,128]{4,3,2,1,0:T(8,128)(2,1)} %get-tuple-element.53), channel_id=1, source_target_pairs={{0,1},{1,0},{2,3},{3,2},{4,5},{5,4},{6,7},{7,6},{8,9},{9,8},{10,11... | collective-permute-start | bytes 2359304 | tf_op jit(solution)/shard_map/ppermute | solution.py:307
  107.0 2.2 %copy-done.1 = bf16[2,8,512,256]{3,2,1,0:T(8,128)(2,1)S(1)} copy-done((bf16[2,8,512,256]{3,2,1,0:T(8,128)(2,1)S(1)}, bf16[2,8,512,256]{3,2,1,0:T(8,128)(2,1)}, u32[]{:S(2)}) %copy-start.1) | copy-done | bytes 4194328
  109.1 4.6 %along_x.1 = (bf16[8,2,2,16,128]{4,3,2,1,0:T(8,128)(2,1)S(1)}, bf16[8,2,2,16,128]{4,3,2,1,0:T(8,128)(2,1)S(1)}, bf16[8,2,2,16,128]{4,3,2,1,0:T(8,128)(2,1)S(1)},...) custom-call(s32[1]{0:T(128)} %bitcast.1.who.me, ...), custom_call_target="tpu_custom_call" | custom-call | flops 1073741824 | bytes 8388608 | tf_op jit(solution)/shard_map/along_x/pallas_call | solution.py:268
  113.8 0.1 collective-permute-start
  113.9 0.4 collective-permute-start.1
  114.4 1.1 collective-permute-start.2
  115.5 3.5 %collective-permute-start.3 = (bf16[8,2,2,16,128]{4,3,2,1,0:T(8,128)(2,1)S(1)}, bf16[8,2,2,16,128]{4,3,2,1,0:T(8,128)(2,1)S(1)}, u32[]{:S(2)}, u32[]{:S(2)}) collective-permute-start(bf16[8,2,2,16,128]{4,3,2,1,0:T(8,128)(2,1)S(1)} %get-tuple-element.35), channel_id=1, source_target_pairs={{0,128},{4,132},{8,136},{12,140},{16,144},{20,148},{24,152},{28,15... | collective-permute-start | bytes 393224 | tf_op jit(solution)/shard_map/ppermute | solution.py:283
  118.9 0.0 collective-permute-done.refs_1_
  118.9 0.2 collective-permute-start.4
  119.1 9.3 %collective-permute-done.1.refs_2_ = bf16[8,2,2,16,128]{4,3,2,1,0:T(8,128)(2,1)S(1)} collective-permute-done((bf16[8,2,2,16,128]{4,3,2,1,0:T(8,128)(2,1)S(1)}, bf16[8,2,2,16,128]{4,3,2,1,0:T(8,128)(2,1)S(1)}, u32[]{:S(2)}, u32[]{:S(2)}) %collective-permute-start.1) | collective-permute-done | bytes 131104 | tf_op jit(solution)/shard_map/ppermute | solution.py:283
  128.4 0.0 collective-permute-start.5
  128.4 0.0 collective-permute-done.2.refs_3_
  128.4 0.0 collective-permute-start.6
  128.4 0.0 collective-permute-done.3.refs_4_
  128.5 0.0 collective-permute-done.4.refs_5_
  128.5 7.3 %collective-permute-done.5.refs_6_ = bf16[8,2,2,16,128]{4,3,2,1,0:T(8,128)(2,1)S(1)} collective-permute-done((bf16[8,2,2,16,128]{4,3,2,1,0:T(8,128)(2,1)S(1)}, bf16[8,2,2,16,128]{4,3,2,1,0:T(8,128)(2,1)S(1)}, u32[]{:S(2)}, u32[]{:S(2)}) %collective-permute-start.5) | collective-permute-done | bytes 131104 | tf_op jit(solution)/shard_map/ppermute | solution.py:283
  135.7 0.0 collective-permute-done.6.refs_7_
  135.7 0.1 regroup.1
  135.8 0.1 collective-permute-start.10
  135.9 2.5 %collective-permute-start.11 = (bf16[8,2,2,16,128]{4,3,2,1,0:T(8,128)(2,1)S(1)}, bf16[8,2,2,16,128]{4,3,2,1,0:T(8,128)(2,1)S(1)}, u32[]{:S(2)}, u32[]{:S(2)}) collective-permute-start(bf16[8,2,2,16,128]{4,3,2,1,0:T(8,128)(2,1)S(1)} %get-tuple-element.44), channel_id=1, source_target_pairs={{0,20},{4,24},{8,28},{12,0},{16,4},{20,8},{24,12},{28,16},{32,52},... | collective-permute-start | bytes 393224 | tf_op jit(solution)/shard_map/ppermute | solution.py:294
  138.4 4.5 %collective-permute-start.12 = (bf16[8,2,2,16,128]{4,3,2,1,0:T(8,128)(2,1)S(1)}, bf16[8,2,2,16,128]{4,3,2,1,0:T(8,128)(2,1)S(1)}, u32[]{:S(2)}, u32[]{:S(2)}) collective-permute-start(bf16[8,2,2,16,128]{4,3,2,1,0:T(8,128)(2,1)S(1)} %get-tuple-element.45), channel_id=1, source_target_pairs={{0,24},{4,28},{8,0},{12,4},{16,8},{20,12},{24,16},{28,20},{32,56},... | collective-permute-start | bytes 393224 | tf_op jit(solution)/shard_map/ppermute | solution.py:294
  142.9 0.0 collective-permute-start.13
  142.9 0.9 collective-permute-done.10.refs_4_
  143.8 0.8 collective-permute-start.7
  144.6 7.3 %collective-permute-done.11.refs_5_ = bf16[8,2,2,16,128]{4,3,2,1,0:T(8,128)(2,1)S(1)} collective-permute-done((bf16[8,2,2,16,128]{4,3,2,1,0:T(8,128)(2,1)S(1)}, bf16[8,2,2,16,128]{4,3,2,1,0:T(8,128)(2,1)S(1)}, u32[]{:S(2)}, u32[]{:S(2)}) %collective-permute-start.11) | collective-permute-done | bytes 131104 | tf_op jit(solution)/shard_map/ppermute | solution.py:294
  152.0 7.3 %collective-permute-done.12.refs_6_ = bf16[8,2,2,16,128]{4,3,2,1,0:T(8,128)(2,1)S(1)} collective-permute-done((bf16[8,2,2,16,128]{4,3,2,1,0:T(8,128)(2,1)S(1)}, bf16[8,2,2,16,128]{4,3,2,1,0:T(8,128)(2,1)S(1)}, u32[]{:S(2)}, u32[]{:S(2)}) %collective-permute-start.12) | collective-permute-done | bytes 131104 | tf_op jit(solution)/shard_map/ppermute | solution.py:294
  159.3 3.0 %collective-permute-done.13.refs_7_ = bf16[8,2,2,16,128]{4,3,2,1,0:T(8,128)(2,1)S(1)} collective-permute-done((bf16[8,2,2,16,128]{4,3,2,1,0:T(8,128)(2,1)S(1)}, bf16[8,2,2,16,128]{4,3,2,1,0:T(8,128)(2,1)S(1)}, u32[]{:S(2)}, u32[]{:S(2)}) %collective-permute-start.13) | collective-permute-done | bytes 131104 | tf_op jit(solution)/shard_map/ppermute | solution.py:294
  162.3 0.0 collective-permute-done.7.refs_1_
  162.3 0.0 collective-permute-done.8.refs_2_
  162.3 5.4 %collective-permute-done.9.refs_3_ = bf16[8,2,2,16,128]{4,3,2,1,0:T(8,128)(2,1)S(1)} collective-permute-done((bf16[8,2,2,16,128]{4,3,2,1,0:T(8,128)(2,1)S(1)}, bf16[8,2,2,16,128]{4,3,2,1,0:T(8,128)(2,1)S(1)}, u32[]{:S(2)}, u32[]{:S(2)}) %collective-permute-start.9) | collective-permute-done | bytes 131104 | tf_op jit(solution)/shard_map/ppermute | solution.py:294
  167.7 0.8 along_y.2
  168.5 6.3 %collective-permute-start.14 = (bf16[2,2,2,128,128]{4,3,2,1,0:T(8,128)(2,1)S(1)}, bf16[2,2,2,128,128]{4,3,2,1,0:T(8,128)(2,1)S(1)}, u32[]{:S(2)}, u32[]{:S(2)}) collective-permute-start(bf16[2,2,2,128,128]{4,3,2,1,0:T(8,128)(2,1)S(1)} %get-tuple-element.48), channel_id=1, source_target_pairs={{0,1},{1,0},{2,3},{3,2},{4,5},{5,4},{6,7},{7,6},{8,9},{9,8},{10,11... | collective-permute-start | bytes 786440 | tf_op jit(solution)/shard_map/ppermute | solution.py:307
  174.8 1.4 join_core.3
  176.2 2.5 %collective-permute-start.17 = (bf16[2,6,128,128]{3,2,1,0:T(8,128)(2,1)S(1)}, bf16[2,6,128,128]{3,2,1,0:T(8,128)(2,1)S(1)}, u32[]{:S(2)}, u32[]{:S(2)}) collective-permute-start(bf16[2,6,128,128]{3,2,1,0:T(8,128)(2,1)S(1)} %get-tuple-element.55), channel_id=1, source_target_pairs={{0,2},{1,3},{2,0},{3,1},{4,6},{5,7},{6,4},{7,5},{8,10},{9,11},{10,... | collective-permute-start | bytes 1179656 | tf_op jit(solution)/shard_map/ppermute | solution.py:316
  178.7 0.1 join_core.2
  178.8 0.6 collective-permute-start.15
  179.4 8.8 %collective-permute-done.17.other = bf16[2,6,128,128]{3,2,1,0:T(8,128)(2,1)S(1)} collective-permute-done((bf16[2,6,128,128]{3,2,1,0:T(8,128)(2,1)S(1)}, bf16[2,6,128,128]{3,2,1,0:T(8,128)(2,1)S(1)}, u32[]{:S(2)}, u32[]{:S(2)}) %collective-permute-start.17) | collective-permute-done | bytes 393248 | tf_op jit(solution)/shard_map/ppermute | solution.py:316
  188.2 1.5 join_far.2
  189.7 1.3 collective-permute-done.15.other
  191.0 0.7 join_far.3
  (12 shorter events, 0.0 us)
Async XLA Ops:
  12.2 82.8 %all-to-all-start = ((bf16[64,2,6,16,128]{4,3,2,1,0:T(8,128)(2,1)}), bf16[64,2,6,16,128]{4,3,2,1,0:T(8,128)(2,1)}, u32[]{:S(2)}, u32[]{:S(2)}) async-start(bf16[64,2,6,16,128]{4,3,2,1,0:T(8,128)(2,1)} %get-tuple-element.51), calls=%async_computation | async-start | bytes 6291456 | tf_op jit(solution)/shard_map/all_to_all | solution.py:267
  26.0 1.6 copy-start.2
  27.6 67.4 %copy-start = (bf16[512,1024]{1,0:T(8,128)(2,1)S(1)}, bf16[512,1024]{1,0:T(8,128)(2,1)}, u32[]{:S(2)}) copy-start(bf16[512,1024]{1,0:T(8,128)(2,1)} %constant.20.clone.refs_9_.table) | copy-start | bytes 3145732
  95.0 12.0 %copy-start.5 = (bf16[256,512]{1,0:T(8,128)(2,1)S(1)}, bf16[256,512]{1,0:T(8,128)(2,1)}, u32[]{:S(2)}) copy-start(bf16[256,512]{1,0:T(8,128)(2,1)} %constant.19.clone.table) | copy-start | bytes 786436
  99.8 0.9 copy-start.3
  100.7 74.1 %collective-permute-start.16 = (bf16[2,2,6,128,128]{4,3,2,1,0:T(8,128)(2,1)}, bf16[2,2,6,128,128]{4,3,2,1,0:T(8,128)(2,1)}, u32[]{:S(2)}, u32[]{:S(2)}) collective-permute-start(bf16[2,2,6,128,128]{4,3,2,1,0:T(8,128)(2,1)} %get-tuple-element.53), channel_id=1, source_target_pairs={{0,1},{1,0},{2,3},{3,2},{4,5},{5,4},{6,7},{7,6},{8,9},{9,8},{10,11... | collective-permute-start | bytes 2359304 | tf_op jit(solution)/shard_map/ppermute | solution.py:307
  107.0 2.2 %copy-start.1 = (bf16[2,8,512,256]{3,2,1,0:T(8,128)(2,1)S(1)}, bf16[2,8,512,256]{3,2,1,0:T(8,128)(2,1)}, u32[]{:S(2)}) copy-start(bf16[2,8,512,256]{3,2,1,0:T(8,128)(2,1)} %get-tuple-element.30.q) | copy-start | bytes 12582916
  113.8 5.1 %collective-permute-start = (bf16[8,2,2,16,128]{4,3,2,1,0:T(8,128)(2,1)S(1)}, bf16[8,2,2,16,128]{4,3,2,1,0:T(8,128)(2,1)S(1)}, u32[]{:S(2)}, u32[]{:S(2)}) collective-permute-start(bf16[8,2,2,16,128]{4,3,2,1,0:T(8,128)(2,1)S(1)} %get-tuple-element.32), channel_id=1, source_target_pairs={{0,32},{4,36},{8,40},{12,44},{16,48},{20,52},{24,56},{28,60},{32,0... | collective-permute-start | bytes 393224 | tf_op jit(solution)/shard_map/ppermute | solution.py:283
  113.9 14.5 %collective-permute-start.1 = (bf16[8,2,2,16,128]{4,3,2,1,0:T(8,128)(2,1)S(1)}, bf16[8,2,2,16,128]{4,3,2,1,0:T(8,128)(2,1)S(1)}, u32[]{:S(2)}, u32[]{:S(2)}) collective-permute-start(bf16[8,2,2,16,128]{4,3,2,1,0:T(8,128)(2,1)S(1)} %get-tuple-element.33), channel_id=1, source_target_pairs={{0,64},{4,68},{8,72},{12,76},{16,80},{20,84},{24,88},{28,92},{32,9... | collective-permute-start | bytes 393224 | tf_op jit(solution)/shard_map/ppermute | solution.py:283
  114.4 14.1 %collective-permute-start.2 = (bf16[8,2,2,16,128]{4,3,2,1,0:T(8,128)(2,1)S(1)}, bf16[8,2,2,16,128]{4,3,2,1,0:T(8,128)(2,1)S(1)}, u32[]{:S(2)}, u32[]{:S(2)}) collective-permute-start(bf16[8,2,2,16,128]{4,3,2,1,0:T(8,128)(2,1)S(1)} %get-tuple-element.34), channel_id=1, source_target_pairs={{0,96},{4,100},{8,104},{12,108},{16,112},{20,116},{24,120},{28,124... | collective-permute-start | bytes 393224 | tf_op jit(solution)/shard_map/ppermute | solution.py:283
  115.5 13.0 %collective-permute-start.3 = (bf16[8,2,2,16,128]{4,3,2,1,0:T(8,128)(2,1)S(1)}, bf16[8,2,2,16,128]{4,3,2,1,0:T(8,128)(2,1)S(1)}, u32[]{:S(2)}, u32[]{:S(2)}) collective-permute-start(bf16[8,2,2,16,128]{4,3,2,1,0:T(8,128)(2,1)S(1)} %get-tuple-element.35), channel_id=1, source_target_pairs={{0,128},{4,132},{8,136},{12,140},{16,144},{20,148},{24,152},{28,15... | collective-permute-start | bytes 393224 | tf_op jit(solution)/shard_map/ppermute | solution.py:283
  118.9 9.5 %collective-permute-start.4 = (bf16[8,2,2,16,128]{4,3,2,1,0:T(8,128)(2,1)S(1)}, bf16[8,2,2,16,128]{4,3,2,1,0:T(8,128)(2,1)S(1)}, u32[]{:S(2)}, u32[]{:S(2)}) collective-permute-start(bf16[8,2,2,16,128]{4,3,2,1,0:T(8,128)(2,1)S(1)} %get-tuple-element.36), channel_id=1, source_target_pairs={{0,160},{4,164},{8,168},{12,172},{16,176},{20,180},{24,184},{28,18... | collective-permute-start | bytes 393224 | tf_op jit(solution)/shard_map/ppermute | solution.py:283
  128.4 7.3 %collective-permute-start.5 = (bf16[8,2,2,16,128]{4,3,2,1,0:T(8,128)(2,1)S(1)}, bf16[8,2,2,16,128]{4,3,2,1,0:T(8,128)(2,1)S(1)}, u32[]{:S(2)}, u32[]{:S(2)}) collective-permute-start(bf16[8,2,2,16,128]{4,3,2,1,0:T(8,128)(2,1)S(1)} %get-tuple-element.37), channel_id=1, source_target_pairs={{0,192},{4,196},{8,200},{12,204},{16,208},{20,212},{24,216},{28,22... | collective-permute-start | bytes 393224 | tf_op jit(solution)/shard_map/ppermute | solution.py:283
  128.4 7.3 %collective-permute-start.6 = (bf16[8,2,2,16,128]{4,3,2,1,0:T(8,128)(2,1)S(1)}, bf16[8,2,2,16,128]{4,3,2,1,0:T(8,128)(2,1)S(1)}, u32[]{:S(2)}, u32[]{:S(2)}) collective-permute-start(bf16[8,2,2,16,128]{4,3,2,1,0:T(8,128)(2,1)S(1)} %get-tuple-element.38), channel_id=1, source_target_pairs={{0,224},{4,228},{8,232},{12,236},{16,240},{20,244},{24,248},{28,25... | collective-permute-start | bytes 393224 | tf_op jit(solution)/shard_map/ppermute | solution.py:283
  135.8 8.0 %collective-permute-start.10 = (bf16[8,2,2,16,128]{4,3,2,1,0:T(8,128)(2,1)S(1)}, bf16[8,2,2,16,128]{4,3,2,1,0:T(8,128)(2,1)S(1)}, u32[]{:S(2)}, u32[]{:S(2)}) collective-permute-start(bf16[8,2,2,16,128]{4,3,2,1,0:T(8,128)(2,1)S(1)} %get-tuple-element.43), channel_id=1, source_target_pairs={{0,16},{4,20},{8,24},{12,28},{16,0},{20,4},{24,8},{28,12},{32,48},... | collective-permute-start | bytes 393224 | tf_op jit(solution)/shard_map/ppermute | solution.py:294
  135.9 16.1 %collective-permute-start.11 = (bf16[8,2,2,16,128]{4,3,2,1,0:T(8,128)(2,1)S(1)}, bf16[8,2,2,16,128]{4,3,2,1,0:T(8,128)(2,1)S(1)}, u32[]{:S(2)}, u32[]{:S(2)}) collective-permute-start(bf16[8,2,2,16,128]{4,3,2,1,0:T(8,128)(2,1)S(1)} %get-tuple-element.44), channel_id=1, source_target_pairs={{0,20},{4,24},{8,28},{12,0},{16,4},{20,8},{24,12},{28,16},{32,52},... | collective-permute-start | bytes 393224 | tf_op jit(solution)/shard_map/ppermute | solution.py:294
  138.4 20.9 %collective-permute-start.12 = (bf16[8,2,2,16,128]{4,3,2,1,0:T(8,128)(2,1)S(1)}, bf16[8,2,2,16,128]{4,3,2,1,0:T(8,128)(2,1)S(1)}, u32[]{:S(2)}, u32[]{:S(2)}) collective-permute-start(bf16[8,2,2,16,128]{4,3,2,1,0:T(8,128)(2,1)S(1)} %get-tuple-element.45), channel_id=1, source_target_pairs={{0,24},{4,28},{8,0},{12,4},{16,8},{20,12},{24,16},{28,20},{32,56},... | collective-permute-start | bytes 393224 | tf_op jit(solution)/shard_map/ppermute | solution.py:294
  142.9 19.4 %collective-permute-start.13 = (bf16[8,2,2,16,128]{4,3,2,1,0:T(8,128)(2,1)S(1)}, bf16[8,2,2,16,128]{4,3,2,1,0:T(8,128)(2,1)S(1)}, u32[]{:S(2)}, u32[]{:S(2)}) collective-permute-start(bf16[8,2,2,16,128]{4,3,2,1,0:T(8,128)(2,1)S(1)} %get-tuple-element.46), channel_id=1, source_target_pairs={{0,28},{4,0},{8,4},{12,8},{16,12},{20,16},{24,20},{28,24},{32,60},... | collective-permute-start | bytes 393224 | tf_op jit(solution)/shard_map/ppermute | solution.py:294
  143.8 18.5 %collective-permute-start.7 = (bf16[8,2,2,16,128]{4,3,2,1,0:T(8,128)(2,1)S(1)}, bf16[8,2,2,16,128]{4,3,2,1,0:T(8,128)(2,1)S(1)}, u32[]{:S(2)}, u32[]{:S(2)}) collective-permute-start(bf16[8,2,2,16,128]{4,3,2,1,0:T(8,128)(2,1)S(1)} %get-tuple-element.40), channel_id=1, source_target_pairs={{0,4},{4,8},{8,12},{12,16},{16,20},{20,24},{24,28},{28,0},{32,36},... | collective-permute-start | bytes 393224 | tf_op jit(solution)/shard_map/ppermute | solution.py:294
  152.0 10.4 %collective-permute-start.8 = (bf16[8,2,2,16,128]{4,3,2,1,0:T(8,128)(2,1)S(1)}, bf16[8,2,2,16,128]{4,3,2,1,0:T(8,128)(2,1)S(1)}, u32[]{:S(2)}, u32[]{:S(2)}) collective-permute-start(bf16[8,2,2,16,128]{4,3,2,1,0:T(8,128)(2,1)S(1)} %get-tuple-element.41), channel_id=1, source_target_pairs={{0,8},{4,12},{8,16},{12,20},{16,24},{20,28},{24,0},{28,4},{32,40},... | collective-permute-start | bytes 393224 | tf_op jit(solution)/shard_map/ppermute | solution.py:294
  159.3 8.4 %collective-permute-start.9 = (bf16[8,2,2,16,128]{4,3,2,1,0:T(8,128)(2,1)S(1)}, bf16[8,2,2,16,128]{4,3,2,1,0:T(8,128)(2,1)S(1)}, u32[]{:S(2)}, u32[]{:S(2)}) collective-permute-start(bf16[8,2,2,16,128]{4,3,2,1,0:T(8,128)(2,1)S(1)} %get-tuple-element.42), channel_id=1, source_target_pairs={{0,12},{4,16},{8,20},{12,24},{16,28},{20,0},{24,4},{28,8},{32,44},... | collective-permute-start | bytes 393224 | tf_op jit(solution)/shard_map/ppermute | solution.py:294
  167.7 7.1 %copy-start.4 = (bf16[2,2,6,128,128]{4,3,2,1,0:T(8,128)(2,1)S(1)}, bf16[2,2,6,128,128]{4,3,2,1,0:T(8,128)(2,1)}, u32[]{:S(2)}) copy-start(bf16[2,2,6,128,128]{4,3,2,1,0:T(8,128)(2,1)} %copy-done.3) | copy-start | bytes 2359300
  168.5 10.2 %collective-permute-start.14 = (bf16[2,2,2,128,128]{4,3,2,1,0:T(8,128)(2,1)S(1)}, bf16[2,2,2,128,128]{4,3,2,1,0:T(8,128)(2,1)S(1)}, u32[]{:S(2)}, u32[]{:S(2)}) collective-permute-start(bf16[2,2,2,128,128]{4,3,2,1,0:T(8,128)(2,1)S(1)} %get-tuple-element.48), channel_id=1, source_target_pairs={{0,1},{1,0},{2,3},{3,2},{4,5},{5,4},{6,7},{7,6},{8,9},{9,8},{10,11... | collective-permute-start | bytes 786440 | tf_op jit(solution)/shard_map/ppermute | solution.py:307
  176.2 12.1 %collective-permute-start.17 = (bf16[2,6,128,128]{3,2,1,0:T(8,128)(2,1)S(1)}, bf16[2,6,128,128]{3,2,1,0:T(8,128)(2,1)S(1)}, u32[]{:S(2)}, u32[]{:S(2)}) collective-permute-start(bf16[2,6,128,128]{3,2,1,0:T(8,128)(2,1)S(1)} %get-tuple-element.55), channel_id=1, source_target_pairs={{0,2},{1,3},{2,0},{3,1},{4,6},{5,7},{6,4},{7,5},{8,10},{9,11},{10,... | collective-permute-start | bytes 1179656 | tf_op jit(solution)/shard_map/ppermute | solution.py:316
  178.8 12.2 %collective-permute-start.15 = (bf16[2,2,128,128]{3,2,1,0:T(8,128)(2,1)S(1)}, bf16[2,2,128,128]{3,2,1,0:T(8,128)(2,1)S(1)}, u32[]{:S(2)}, u32[]{:S(2)}) collective-permute-start(bf16[2,2,128,128]{3,2,1,0:T(8,128)(2,1)S(1)} %get-tuple-element.50), channel_id=1, source_target_pairs={{0,2},{1,3},{2,0},{3,1},{4,6},{5,7},{6,4},{7,5},{8,10},{9,11},{10,... | collective-permute-start | bytes 393224 | tf_op jit(solution)/shard_map/ppermute | solution.py:316
